TPU v7x, 32 devices: a whole 2x2x4 slice. The times are simulated.
32 devices in a mesh: dp: 4 (over y, x), fsdp: 8 (over z, core).
Axes of the slice: x: 2, y: 2, z: 4, core: 2. Of those that a mesh axis runs over, the one named last changes fastest.
Arguments:
- text_in: bfloat16 [16384, 768], P(('dp', 'fsdp')), may hold values from -6 to 6
- layout_in: bfloat16 [16384, 192], P(('dp', 'fsdp')), may hold values from -6 to 6
- lengths: int32 [32], P(('dp', 'fsdp')), may hold values from 1 to 512, as said below
- attn_text: bfloat16 [768, 3072], P(None, ('dp', 'fsdp'))
- up_text: bfloat16 [768, 3072], P(None, ('dp', 'fsdp')), may hold values from -0.21875 to 0.21875
- down_text: bfloat16 [3072, 768], P(('dp', 'fsdp')), may hold values from -0.109375 to 0.109375
- attn_layout: bfloat16 [192, 768], P(None, ('dp', 'fsdp'))
- up_layout: bfloat16 [192, 768], P(None, ('dp', 'fsdp')), may hold values from -0.4375 to 0.4375
- down_layout: bfloat16 [768, 192], P(('dp', 'fsdp')), may hold values from -0.21875 to 0.21875
- norm_params: bfloat16 [3840], P(('dp', 'fsdp'))
- grad_text: bfloat16 [16384, 768], P(('dp', 'fsdp')), may hold values from -6 to 6
- grad_layout: bfloat16 [16384, 192], P(('dp', 'fsdp')), may hold values from -6 to 6
Outputs:
- text_out: bfloat16 [16384, 768], P(('dp', 'fsdp'))
- layout_out: bfloat16 [16384, 192], P(('dp', 'fsdp'))
- text_in_grad: bfloat16 [16384, 768], P(('dp', 'fsdp'))
- layout_in_grad: bfloat16 [16384, 192], P(('dp', 'fsdp'))
- attn_text_grad: float32 [768, 3072], P(None, ('dp', 'fsdp'))
- up_text_grad: float32 [768, 3072], P(None, ('dp', 'fsdp'))
- down_text_grad: float32 [3072, 768], P(('dp', 'fsdp'))
- attn_layout_grad: float32 [192, 768], P(None, ('dp', 'fsdp'))
- up_layout_grad: float32 [192, 768], P(None, ('dp', 'fsdp'))
- down_layout_grad: float32 [768, 192], P(('dp', 'fsdp'))
- norm_grad: float32 [3840], P(('dp', 'fsdp'))
Inputs may be any that keep to these rules, and one draw needn't show every extreme that they name: Tokens held by each page slot; the first lengths[s] places of slot s are real tokens, the rest padding; at least one slot holds 512 tokens in every draw.
All inputs are finite; a program needn't handle non-finite values.
Results may differ from a plain program's by a relative error of at most 0.014.
Values may be sent and summed in bfloat16 or wider, within the bound.
A program may use at most 256 MiB of HBM per device.

v0:
```python
import jax
import jax.numpy as jnp
from jax import lax
from jax.sharding import PartitionSpec as P

HEADS = 12
PAGE = 512


EPSILON = 1e-05
NEG_FILL = -1000000000.0


def layer_norm(hidden, gain, shift):
    centre = jnp.mean(hidden, axis=-1, keepdims=True)
    centred = hidden - centre
    spread = jnp.mean(centred * centred, axis=-1, keepdims=True)
    return centred * lax.rsqrt(spread + EPSILON) * gain + shift


def gelu_exact(value):
    return jax.nn.gelu(value, approximate=False)


def owner_rows(matrix, owners):
    row_count, col_count = matrix.shape
    width = col_count // owners
    blocks = matrix.reshape(row_count, owners, width)
    return jnp.transpose(blocks, (1, 0, 2)).reshape(owners * row_count, width)


def split_heads(projected, slot_count):
    model_width = projected.shape[1] // 3
    shaped = projected.reshape(slot_count, PAGE, 3, HEADS, model_width // HEADS)
    return (shaped[:, :, 0], shaped[:, :, 1], shaped[:, :, 2])


def score_block(query_text, key_text, query_layout, key_layout, length):
    raw_text = jnp.einsum("qhd,khd->hqk", query_text, key_text, preferred_element_type=jnp.float32)
    raw_layout = jnp.einsum(
        "qhd,khd->hqk", query_layout, key_layout, preferred_element_type=jnp.float32
    )
    scores = raw_text * query_text.shape[-1] ** (-0.5) + raw_layout * query_layout.shape[-1] ** (
        -0.5
    )
    valid = jnp.arange(scores.shape[-1], dtype=jnp.int32) < length
    return jnp.where(valid[None, None, :], scores, NEG_FILL)


def forward_slot(state_in, pieces):
    query_text, key_text, value_text, query_layout, key_layout, value_layout, length = pieces
    scores = score_block(query_text, key_text, query_layout, key_layout, length)
    row_top = jnp.max(scores, axis=-1, keepdims=True)
    log_total = row_top + jnp.log(jnp.sum(jnp.exp(scores - row_top), axis=-1, keepdims=True))
    attn_probs = jnp.exp(scores - log_total).astype(jnp.bfloat16)
    context_text = jnp.einsum(
        "hqk,khd->qhd", attn_probs, value_text, preferred_element_type=jnp.float32
    ).astype(jnp.bfloat16)
    context_layout = jnp.einsum(
        "hqk,khd->qhd", attn_probs, value_layout, preferred_element_type=jnp.float32
    ).astype(jnp.bfloat16)
    return (state_in, (context_text, context_layout, log_total))


def backward_slot(state_in, pieces):
    (
        query_text,
        key_text,
        value_text,
        query_layout,
        key_layout,
        value_layout,
        length,
        log_total,
        grad_ctx_text,
        grad_ctx_layout,
    ) = pieces
    scores = score_block(query_text, key_text, query_layout, key_layout, length)
    exact_probs = jnp.exp(scores - log_total)
    attn_probs = exact_probs.astype(jnp.bfloat16)
    value_text_grad = jnp.einsum(
        "hqk,qhd->khd", attn_probs, grad_ctx_text, preferred_element_type=jnp.float32
    ).astype(jnp.bfloat16)
    value_layout_grad = jnp.einsum(
        "hqk,qhd->khd", attn_probs, grad_ctx_layout, preferred_element_type=jnp.float32
    ).astype(jnp.bfloat16)
    prob_grad = jnp.einsum(
        "qhd,khd->hqk", grad_ctx_text, value_text, preferred_element_type=jnp.float32
    )
    prob_grad = prob_grad + jnp.einsum(
        "qhd,khd->hqk", grad_ctx_layout, value_layout, preferred_element_type=jnp.float32
    )
    score_grad = exact_probs * (
        prob_grad - jnp.sum(prob_grad * exact_probs, axis=-1, keepdims=True)
    )
    text_score_grad = (score_grad * query_text.shape[-1] ** (-0.5)).astype(jnp.bfloat16)
    layout_score_grad = (score_grad * query_layout.shape[-1] ** (-0.5)).astype(jnp.bfloat16)
    query_text_grad = jnp.einsum(
        "hqk,khd->qhd", text_score_grad, key_text, preferred_element_type=jnp.float32
    ).astype(jnp.bfloat16)
    key_text_grad = jnp.einsum(
        "hqk,qhd->khd", text_score_grad, query_text, preferred_element_type=jnp.float32
    ).astype(jnp.bfloat16)
    query_layout_grad = jnp.einsum(
        "hqk,khd->qhd", layout_score_grad, key_layout, preferred_element_type=jnp.float32
    ).astype(jnp.bfloat16)
    key_layout_grad = jnp.einsum(
        "hqk,qhd->khd", layout_score_grad, query_layout, preferred_element_type=jnp.float32
    ).astype(jnp.bfloat16)
    return (
        state_in,
        (
            query_text_grad,
            key_text_grad,
            value_text_grad,
            query_layout_grad,
            key_layout_grad,
            value_layout_grad,
        ),
    )


def stream_tail(stream_in, context, out_weight, up_weight, down_weight, norm_part):
    branch = jnp.dot(context, out_weight, preferred_element_type=jnp.float32)
    middle, first_back = jax.vjp(
        layer_norm, stream_in.astype(jnp.float32) + branch, norm_part[0], norm_part[1]
    )
    middle_low = middle.astype(jnp.bfloat16)
    inner = jnp.dot(middle_low, up_weight, preferred_element_type=jnp.float32)
    activated, gelu_back = jax.vjp(gelu_exact, inner)
    activated_low = activated.astype(jnp.bfloat16)
    second = jnp.dot(activated_low, down_weight, preferred_element_type=jnp.float32)
    result, second_back = jax.vjp(layer_norm, middle + second, norm_part[2], norm_part[3])
    return (
        result.astype(jnp.bfloat16),
        (first_back, middle_low, gelu_back, activated_low, second_back),
    )


def tail_backward(saved, grad_out, up_weight, down_weight):
    first_back, middle_low, gelu_back, activated_low, second_back = saved
    grad_second, gain_two, shift_two = second_back(grad_out.astype(jnp.float32))
    second_low = grad_second.astype(jnp.bfloat16)
    down_grad = jnp.einsum(
        "rf,rd->fd", activated_low, second_low, preferred_element_type=jnp.float32
    )
    grad_active = jnp.einsum(
        "rd,fd->rf", second_low, down_weight, preferred_element_type=jnp.float32
    )
    inner_low = gelu_back(grad_active)[0].astype(jnp.bfloat16)
    up_grad = jnp.einsum("rd,rf->df", middle_low, inner_low, preferred_element_type=jnp.float32)
    grad_middle = grad_second + jnp.einsum(
        "rf,df->rd", inner_low, up_weight, preferred_element_type=jnp.float32
    )
    grad_first, gain_one, shift_one = first_back(grad_middle)
    return (
        grad_first,
        up_grad,
        down_grad,
        jnp.concatenate([gain_one, shift_one, gain_two, shift_two]),
    )


def per_device(
    text_in,
    layout_in,
    lengths,
    attn_text,
    up_text,
    down_text,
    attn_layout,
    up_layout,
    down_layout,
    norm_params,
    grad_text,
    grad_layout,
):
    text_width = text_in.shape[1]
    layout_width = layout_in.shape[1]
    slot_count = lengths.shape[0]
    owners = lax.axis_size(("dp", "fsdp"))
    text_attn, text_up, text_down = (
        lax.all_gather(attn_text, ("dp", "fsdp"), axis=1, tiled=True),
        lax.all_gather(up_text, ("dp", "fsdp"), axis=1, tiled=True),
        lax.all_gather(down_text, ("dp", "fsdp"), axis=0, tiled=True),
    )
    layout_attn, layout_up, layout_down, norm_full = (
        lax.all_gather(attn_layout, ("dp", "fsdp"), axis=1, tiled=True),
        lax.all_gather(up_layout, ("dp", "fsdp"), axis=1, tiled=True),
        lax.all_gather(down_layout, ("dp", "fsdp"), axis=0, tiled=True),
        lax.all_gather(norm_params, ("dp", "fsdp"), axis=0, tiled=True),
    )
    norm_floats = norm_full.astype(jnp.float32)
    text_norms = norm_floats[: 4 * text_width].reshape(4, text_width)
    layout_norms = norm_floats[4 * text_width :].reshape(4, layout_width)
    text_heads = split_heads(
        jnp.dot(text_in, text_attn[:, : 3 * text_width], preferred_element_type=jnp.float32).astype(
            jnp.bfloat16
        ),
        slot_count,
    )
    layout_heads = split_heads(
        jnp.dot(
            layout_in, layout_attn[:, : 3 * layout_width], preferred_element_type=jnp.float32
        ).astype(jnp.bfloat16),
        slot_count,
    )
    scanned = (
        text_heads[0],
        text_heads[1],
        text_heads[2],
        layout_heads[0],
        layout_heads[1],
        layout_heads[2],
        lengths,
    )
    unused_state, slot_outputs = lax.scan(forward_slot, 0, scanned)
    context_text = slot_outputs[0].reshape(-1, text_width)
    context_layout = slot_outputs[1].reshape(-1, layout_width)
    log_totals = slot_outputs[2]
    text_out, text_saved = stream_tail(
        text_in, context_text, text_attn[:, 3 * text_width :], text_up, text_down, text_norms
    )
    layout_out, layout_saved = stream_tail(
        layout_in,
        context_layout,
        layout_attn[:, 3 * layout_width :],
        layout_up,
        layout_down,
        layout_norms,
    )
    back_text = (
        lax.all_gather(attn_text, ("dp", "fsdp"), axis=1, tiled=True),
        lax.all_gather(up_text, ("dp", "fsdp"), axis=1, tiled=True),
        lax.all_gather(down_text, ("dp", "fsdp"), axis=0, tiled=True),
    )
    back_layout = (
        lax.all_gather(attn_layout, ("dp", "fsdp"), axis=1, tiled=True),
        lax.all_gather(up_layout, ("dp", "fsdp"), axis=1, tiled=True),
        lax.all_gather(down_layout, ("dp", "fsdp"), axis=0, tiled=True),
    )
    first_text, text_up_grad, text_down_grad, text_norm_grad = tail_backward(
        text_saved, grad_text, back_text[1], back_text[2]
    )
    first_layout, layout_up_grad, layout_down_grad, layout_norm_grad = tail_backward(
        layout_saved, grad_layout, back_layout[1], back_layout[2]
    )
    norm_total_grad = jnp.concatenate([text_norm_grad, layout_norm_grad])
    branch_text_low = first_text.astype(jnp.bfloat16)
    branch_layout_low = first_layout.astype(jnp.bfloat16)
    out_text_grad = jnp.einsum(
        "rc,rd->cd", context_text, branch_text_low, preferred_element_type=jnp.float32
    )
    out_layout_grad = jnp.einsum(
        "rc,rd->cd", context_layout, branch_layout_low, preferred_element_type=jnp.float32
    )
    ctx_text_grad = jnp.einsum(
        "rd,cd->rc",
        branch_text_low,
        back_text[0][:, 3 * text_width :],
        preferred_element_type=jnp.float32,
    ).astype(jnp.bfloat16)
    ctx_layout_grad = jnp.einsum(
        "rd,cd->rc",
        branch_layout_low,
        back_layout[0][:, 3 * layout_width :],
        preferred_element_type=jnp.float32,
    ).astype(jnp.bfloat16)
    back_scanned = (
        text_heads[0],
        text_heads[1],
        text_heads[2],
        layout_heads[0],
        layout_heads[1],
        layout_heads[2],
        lengths,
        log_totals,
        ctx_text_grad.reshape(text_heads[0].shape),
        ctx_layout_grad.reshape(layout_heads[0].shape),
    )
    unused_back, slot_grads = lax.scan(backward_slot, 0, back_scanned)
    text_proj_grad = jnp.stack([slot_grads[0], slot_grads[1], slot_grads[2]], axis=2).reshape(
        -1, 3 * text_width
    )
    layout_proj_grad = jnp.stack([slot_grads[3], slot_grads[4], slot_grads[5]], axis=2).reshape(
        -1, 3 * layout_width
    )
    text_in_grad = (
        first_text
        + jnp.einsum(
            "re,de->rd",
            text_proj_grad,
            back_text[0][:, : 3 * text_width],
            preferred_element_type=jnp.float32,
        )
    ).astype(jnp.bfloat16)
    layout_in_grad = (
        first_layout
        + jnp.einsum(
            "re,de->rd",
            layout_proj_grad,
            back_layout[0][:, : 3 * layout_width],
            preferred_element_type=jnp.float32,
        )
    ).astype(jnp.bfloat16)
    text_attn_grad = jnp.concatenate(
        [
            jnp.einsum("rd,re->de", text_in, text_proj_grad, preferred_element_type=jnp.float32),
            out_text_grad,
        ],
        axis=1,
    )
    layout_attn_grad = jnp.concatenate(
        [
            jnp.einsum(
                "rd,re->de", layout_in, layout_proj_grad, preferred_element_type=jnp.float32
            ),
            out_layout_grad,
        ],
        axis=1,
    )
    attn_text_grad, up_text_grad, down_text_grad = (
        lax.psum_scatter(
            owner_rows(text_attn_grad, owners), ("dp", "fsdp"), scatter_dimension=0, tiled=True
        ),
        lax.psum_scatter(
            owner_rows(text_up_grad, owners), ("dp", "fsdp"), scatter_dimension=0, tiled=True
        ),
        lax.psum_scatter(text_down_grad, ("dp", "fsdp"), scatter_dimension=0, tiled=True),
    )
    attn_layout_grad, up_layout_grad, down_layout_grad, norm_grad = (
        lax.psum_scatter(
            owner_rows(layout_attn_grad, owners), ("dp", "fsdp"), scatter_dimension=0, tiled=True
        ),
        lax.psum_scatter(
            owner_rows(layout_up_grad, owners), ("dp", "fsdp"), scatter_dimension=0, tiled=True
        ),
        lax.psum_scatter(layout_down_grad, ("dp", "fsdp"), scatter_dimension=0, tiled=True),
        lax.psum_scatter(norm_total_grad, ("dp", "fsdp"), scatter_dimension=0, tiled=True),
    )
    return (
        text_out,
        layout_out,
        text_in_grad,
        layout_in_grad,
        attn_text_grad,
        up_text_grad,
        down_text_grad,
        attn_layout_grad,
        up_layout_grad,
        down_layout_grad,
        norm_grad,
    )


def solution(mesh):
    in_specs = (
        P(("dp", "fsdp"), None),
        P(("dp", "fsdp"), None),
        P(("dp", "fsdp")),
        P(None, ("dp", "fsdp")),
        P(None, ("dp", "fsdp")),
        P(("dp", "fsdp"), None),
        P(None, ("dp", "fsdp")),
        P(None, ("dp", "fsdp")),
        P(("dp", "fsdp"), None),
        P(("dp", "fsdp")),
        P(("dp", "fsdp"), None),
        P(("dp", "fsdp"), None),
    )
    out_specs = (
        P(("dp", "fsdp"), None),
        P(("dp", "fsdp"), None),
        P(("dp", "fsdp"), None),
        P(("dp", "fsdp"), None),
        P(None, ("dp", "fsdp")),
        P(None, ("dp", "fsdp")),
        P(("dp", "fsdp"), None),
        P(None, ("dp", "fsdp")),
        P(None, ("dp", "fsdp")),
        P(("dp", "fsdp"), None),
        P(("dp", "fsdp")),
    )
    return jax.shard_map(
        per_device, mesh=mesh, in_specs=in_specs, out_specs=out_specs, check_vma=False
    )
```

profile of v0, /device:TPU:0, one launch (start us, length us, event | category | flops | bytes accessed | tf_op | source)
XLA Modules:
  0.0 1104.9 jit_solution(12003192227463762027)
XLA Ops:
  10.3 42.9 %all-reduce = bf16[3840]{0:T(1024)(128)(2,1)S(1)} all-reduce(bf16[3840]{0:T(1024)(128)(2,1)S(1)} %dynamic-update-slice), channel_id=1, replica_groups=mesh['dp'=4,'fsdp'=8] {'dp','fsdp'}, use_global_device_ids=true, to_apply=%add | all-reduce | flops 3840 | bytes 15360
  54.5 43.2 %all_gather.28 = bf16[192,768]{0,1:T(8,128)(2,1)S(1)} all-gather(bf16[192,24]{0,1:T(8,128)(2,1)} %param.18), channel_id=1, replica_groups=mesh['dp'=4,'fsdp'=8] {'dp','fsdp'}, dimensions={1}, use_global_device_ids=true | all-gather | bytes 304128 | tf_op jit(solution)/shard_map/all_gather | solution.py:188
  98.4 42.2 %all_gather.32 = bf16[192,768]{0,1:T(8,128)(2,1)} all-gather(bf16[192,24]{0,1:T(8,128)(2,1)} %param.19), channel_id=1, replica_groups=mesh['dp'=4,'fsdp'=8] {'dp','fsdp'}, dimensions={1}, use_global_device_ids=true | all-gather | bytes 304128 | tf_op jit(solution)/shard_map/all_gather | solution.py:189
  140.6 43.5 %all_gather.33 = bf16[768,192]{1,0:T(8,128)(2,1)} all-gather(bf16[24,192]{1,0:T(8,128)(2,1)} %param.20), channel_id=1, replica_groups=mesh['dp'=4,'fsdp'=8] {'dp','fsdp'}, dimensions={0}, use_global_device_ids=true | all-gather | bytes 304128 | tf_op jit(solution)/shard_map/all_gather | solution.py:190
  194.1 6.4 fusion.79
  200.5 6.8 fusion.123
  211.9 6.5 fusion.2
  239.7 7.3 fusion.87
  247.1 19.4 %multiply_convert_fusion.2 = (bf16[512,3072]{1,0:T(8,128)(2,1)}, f32[512,3072]{1,0:T(8,128)}, f32[512,3072]{1,0:T(8,128)}) fusion(bf16[768,3072]{0,1:T(8,128)(2,1)} %all-gather.6.cloned.1.call-done, f32[512,768]{1,0:T(8,128)S(1)} %copy-done.9, f32[768]{0:T(1024)S(1)} %copy-done.70, f32[768]{0:T(1024)S(1)} %copy-done.56, f32[512]{0:T(512)S(1)} %copy-done.60, ...), kind=kOutput, calls=%fused_computation.14 | convolution fusion | flops 2520121344 | bytes 22030336 | tf_op jit(solution)/shard_map/dot_general | solution.py:129
  275.8 8.9 add_convert_fusion
  297.5 7.6 fusion.78
  305.1 25.5 %fusion.70 = bf16[1,512,1,12,16]{1,4,3,2,0:T(8,128)(2,1)} fusion(f32[12,512,512]{1,2,0:T(8,128)} %copy-done.1, f32[12,512]{1,0:T(8,128)S(1)} %log_add_fusion, f32[12,512,512]{1,2,0:T(8,128)} %fusion.78, f32[12,512,512]{1,2,0:T(8,128)} %fusion.87, bf16[1,512,3,12,16]{1,4,3,2,0:T(8,128)(2,1)} %bitcast.148), kind=kOutput, calls=%fused_computation.100 | convolution fusion | flops 129079808 | bytes 75956224 | tf_op jit(solution)/shard_map/while/body/eval_jaxpr/hqk,qhd->khd/dot_general | solution.py:107
  330.6 25.5 %fusion.73 = bf16[1,512,1,12,16]{1,4,3,2,0:T(8,128)(2,1)} fusion(f32[12,512,512]{1,2,0:T(8,128)} %copy-done.1, f32[12,512]{1,0:T(8,128)S(1)} %log_add_fusion, f32[12,512,512]{1,2,0:T(8,128)} %fusion.78, f32[12,512,512]{1,2,0:T(8,128)} %fusion.87, bf16[1,512,3,12,16]{1,4,3,2,0:T(8,128)(2,1)} %bitcast.149), kind=kOutput, calls=%fused_computation.101 | convolution fusion | flops 129079808 | bytes 75956224 | tf_op jit(solution)/shard_map/while/body/eval_jaxpr/hqk,khd->qhd/dot_general | solution.py:104
  368.4 27.3 %fusion.55 = bf16[1,512,1,12,64]{1,4,3,2,0:T(8,128)(2,1)} fusion(f32[12,512,512]{1,2,0:T(8,128)} %copy-done.1, f32[12,512]{1,0:T(8,128)S(1)} %log_add_fusion, f32[12,512,512]{1,2,0:T(8,128)} %fusion.78, f32[12,512,512]{1,2,0:T(8,128)} %fusion.87, bf16[1,512,3,12,64]{1,4,3,2,0:T(8,128)(2,1)S(1)} %bitcast.132), kind=kOutput, calls=%fused_computation.85 | convolution fusion | flops 431364608 | bytes 77135872 | tf_op jit(solution)/shard_map/while/body/eval_jaxpr/hqk,qhd->khd/dot_general | solution.py:101
  395.7 30.0 %fusion.58 = bf16[1,512,1,12,64]{1,4,3,2,0:T(8,128)(2,1)} fusion(f32[12,512,512]{1,2,0:T(8,128)} %copy-done.1, f32[12,512]{1,0:T(8,128)S(1)} %log_add_fusion, f32[12,512,512]{1,2,0:T(8,128)} %fusion.78, f32[12,512,512]{1,2,0:T(8,128)} %fusion.87, bf16[1,512,3,12,64]{1,4,3,2,0:T(8,128)(2,1)S(1)} %bitcast.133), kind=kOutput, calls=%fused_computation.86 | convolution fusion | flops 431364608 | bytes 77135872 | tf_op jit(solution)/shard_map/while/body/eval_jaxpr/hqk,khd->qhd/dot_general | solution.py:98
  445.9 8.0 pad_maximum_fusion
  453.9 8.3 copy.106
  473.6 8.8 fusion.104
  483.2 37.7 %all-reduce.1 = f32[3840]{0:T(1024)S(1)} all-reduce(f32[3840]{0:T(1024)S(1)} %concatenate.11), channel_id=8, replica_groups=mesh['dp'=4,'fsdp'=8] {'dp','fsdp'}, use_global_device_ids=true, to_apply=%region_33.34.clone | all-reduce | flops 3840 | bytes 30720
  530.5 41.2 %reduce-scatter.21.cloned.1.call-done = f32[192,24]{1,0:T(8,128)} async-done(((f32[6144,24]{1,0:T(8,128)}), f32[192,24]{1,0:T(8,128)}) %reduce-scatter.21.cloned.1.call-update) | async-done | bytes 18448
  573.3 99.3 %reduce-scatter.17.cloned.1.call-done = f32[24,192]{1,0:T(8,128)} async-done(((f32[768,192]{1,0:T(8,128)}), f32[24,192]{1,0:T(8,128)}) %reduce-scatter.17.cloned.1.call-update) | async-done | bytes 18448 | tf_op jit(solution)/shard_map/reduce_scatter | solution.py:338
  672.5 141.8 %reduce-scatter.11.cloned.1.call-done = f32[768,96]{0,1:T(8,128)} async-done(((f32[24576,96]{0,1:T(8,128)}), f32[768,96]{0,1:T(8,128)}) %reduce-scatter.11.cloned.1.call-update) | async-done | bytes 294928 | tf_op jit(solution)/shard_map/reduce_scatter | solution.py:323
  814.4 141.9 %reduce-scatter.13.cloned.1.call-done = f32[768,96]{0,1:T(8,128)} async-done(((f32[24576,96]{0,1:T(8,128)}), f32[768,96]{0,1:T(8,128)}) %reduce-scatter.13.cloned.1.call-update) | async-done | bytes 294928 | tf_op jit(solution)/shard_map/reduce_scatter | solution.py:326
  956.2 141.7 %reduce-scatter.15.cloned.1.call-done = f32[96,768]{1,0:T(8,128)} async-done(((f32[3072,768]{1,0:T(8,128)}), f32[96,768]{1,0:T(8,128)}) %reduce-scatter.15.cloned.1.call-update) | async-done | bytes 294928 | tf_op jit(solution)/shard_map/reduce_scatter | solution.py:329
  (250 shorter events, 117.3 us)
Async XLA Ops:
  7.2 178.2 %all-gather.4.cloned.1.call-start = ((), (), s32[]{:S(2)}) async-start(), calls=%async_computation.6 | async-start | bytes 4866048 | tf_op jit(solution)/shard_map/all_gather | solution.py:183
  7.9 239.1 %all-gather.6.cloned.1.call-start = ((), (), s32[]{:S(2)}) async-start(), calls=%async_computation.7 | async-start | bytes 4866048 | tf_op jit(solution)/shard_map/all_gather | solution.py:184
  8.7 257.8 %all-gather.8.cloned.1.call-start = ((), (), s32[]{:S(2)}) async-start(), calls=%async_computation.8 | async-start | bytes 4866048 | tf_op jit(solution)/shard_map/all_gather | solution.py:185
  9.4 519.5 %reduce-scatter.19.cloned.1.call-start = ((), (), s32[]{:S(2)}) async-start(), calls=%async_computation.13 | async-start | bytes 3244032
  97.7 86.4 %copy-start.19 = (bf16[192,768]{0,1:T(8,128)(2,1)}, bf16[192,768]{0,1:T(8,128)(2,1)S(1)}, u32[]{:S(2)}) copy-start(bf16[192,768]{0,1:T(8,128)(2,1)S(1)} %all_gather.28) | copy-start | bytes 884740
  185.3 15.1 %copy-start.18 = (bf16[512,576]{0,1:T(8,128)(2,1)}, bf16[512,576]{0,1:T(8,128)(2,1)S(1)}, u32[]{:S(2)}) copy-start(bf16[512,576]{0,1:T(8,128)(2,1)S(1)} %convolution_convert_fusion.4) | copy-start | bytes 1769476
  218.4 18.8 %copy-start = (bf16[12,512,512]{1,2,0:T(8,128)(2,1)}, bf16[12,512,512]{1,2,0:T(8,128)(2,1)S(1)}, u32[]{:S(2)}) copy-start(bf16[12,512,512]{1,2,0:T(8,128)(2,1)S(1)} %fusion.2) | copy-start | bytes 18874372
  221.1 14.9 %copy-start.39 = (f32[512]{0:T(512)}, f32[512]{0:T(512)S(1)}, u32[]{:S(2)}) copy-start(f32[512]{0:T(512)S(1)} %fusion.94) | copy-start | bytes 6148
  274.1 10.5 slice-start
  290.9 14.2 %copy-start.62 = (f32[512]{0:T(512)}, f32[512]{0:T(512)S(1)}, u32[]{:S(2)}) copy-start(f32[512]{0:T(512)S(1)} %negate_multiply_fusion.4) | copy-start | bytes 6148
  330.6 25.5 %copy-start.12 = (f32[512,192]{0,1:T(8,128)S(1)}, f32[512,192]{0,1:T(8,128)}, u32[]{:S(2)}) copy-start(f32[512,192]{0,1:T(8,128)} %copy-done.11) | copy-start | bytes 1179652
  330.6 25.5 %copy-start.26 = (bf16[12,16,512]{2,1,0:T(8,128)(2,1)S(1)}, bf16[12,16,512]{2,1,0:T(8,128)(2,1)}, u32[]{:S(2)}) copy-start(bf16[12,16,512]{2,1,0:T(8,128)(2,1)} %copy-done.25) | copy-start | bytes 589828
  330.6 25.5 %copy-start.36 = (f32[512]{0:T(512)S(1)}, f32[512]{0:T(512)}, u32[]{:S(2)}) copy-start(f32[512]{0:T(512)} %copy-done.35) | copy-start | bytes 6148
  330.6 25.8 %copy-start.40 = (f32[512]{0:T(512)S(1)}, f32[512]{0:T(512)}, u32[]{:S(2)}) copy-start(f32[512]{0:T(512)} %copy-done.39) | copy-start | bytes 6148
  330.6 25.8 %copy-start.55 = (f32[192]{0:T(256)S(1)}, f32[192]{0:T(256)}, u32[]{:S(2)}) copy-start(f32[192]{0:T(256)} %get-tuple-element.123) | copy-start | bytes 2308
  330.6 25.8 %copy-start.59 = (f32[192]{0:T(256)S(1)}, f32[192]{0:T(256)}, u32[]{:S(2)}) copy-start(f32[192]{0:T(256)} %get-tuple-element.124) | copy-start | bytes 2308
  366.0 205.7 %reduce-scatter.21.cloned.1.call-start = ((), (), s32[]{:S(2)}) async-start(), calls=%async_computation.14 | async-start | bytes 3244032
  395.7 30.0 %copy-start.5 = (bf16[512,768]{0,1:T(8,128)(2,1)S(1)}, bf16[512,768]{0,1:T(8,128)(2,1)}, u32[]{:S(2)}) copy-start(bf16[512,768]{0,1:T(8,128)(2,1)} %copy.74) | copy-start | bytes 2359300
  431.4 241.1 %reduce-scatter.17.cloned.1.call-start = ((), (), s32[]{:S(2)}) async-start(), calls=%async_computation.12 | async-start | bytes 811008 | tf_op jit(solution)/shard_map/reduce_scatter | solution.py:338
  442.1 372.3 %reduce-scatter.11.cloned.1.call-start = ((), (), s32[]{:S(2)}) async-start(), calls=%async_computation.9 | async-start | bytes 9732096 | tf_op jit(solution)/shard_map/reduce_scatter | solution.py:323
  462.3 493.9 %reduce-scatter.13.cloned.1.call-start = ((), (), s32[]{:S(2)}) async-start(), calls=%async_computation.10 | async-start | bytes 9732096 | tf_op jit(solution)/shard_map/reduce_scatter | solution.py:326
  472.9 625.0 %reduce-scatter.15.cloned.1.call-start = ((), (), s32[]{:S(2)}) async-start(), calls=%async_computation.11 | async-start | bytes 9732096 | tf_op jit(solution)/shard_map/reduce_scatter | solution.py:329
  482.5 39.0 %copy-start.13 = (f32[512,192]{0,1:T(8,128)S(1)}, f32[512,192]{0,1:T(8,128)}, u32[]{:S(2)}) copy-start(f32[512,192]{0,1:T(8,128)} %copy-done.11) | copy-start | bytes 1179652
  482.5 39.0 %copy-start.17 = (bf16[1,512,3,12,16]{1,4,3,2,0:T(8,128)(2,1)S(1)}, bf16[1,512,3,12,16]{1,4,3,2,0:T(8,128)(2,1)}, u32[]{:S(2)}) copy-start(bf16[1,512,3,12,16]{1,4,3,2,0:T(8,128)(2,1)} %copy-done.16) | copy-start | bytes 1769476
  (64 other events, 224.3 us)
Sparse Core Ops, SparseCore 0:
  11.0 67.0 all-gather.3
  81.1 62.7 all-gather.5
  147.0 62.8 all-gather.7
  366.1 99.0 reduce-scatter.18
  470.5 101.1 reduce-scatter.20
  577.2 95.2 reduce-scatter.16
  679.0 135.2 reduce-scatter.10
  820.8 135.3 reduce-scatter.12
  962.7 135.1 reduce-scatter.14
where the time goes:
time: 1110 us; the launch traced here: 1100 us
  waiting for transfers between devices  568 us (51%)
  matrix products  244 us (22%)
  blocking collectives  210 us (19%)
  local copies, waits for them, and re-layouts  39.4 us (4%)
  other arithmetic  27.1 us (2%)
  between operations  15.9 us (1%)
    reduce_scatter x1, waiting for transfers between devices, per_device(): lax.psum_scatter(owner_rows(text_up_grad, owners), ('dp', 'fsdp'), scatte...  142 us
    reduce_scatter x1, waiting for transfers between devices, per_device(): lax.psum_scatter(owner_rows(text_attn_grad, owners), ('dp', 'fsdp'), scat...  142 us
    reduce_scatter x1, waiting for transfers between devices, per_device(): lax.psum_scatter(text_down_grad, ('dp', 'fsdp'), scatter_dimension=0, til...  142 us
    reduce_scatter x1, waiting for transfers between devices, per_device(): lax.psum_scatter(layout_down_grad, ('dp', 'fsdp'), scatter_dimension=0, t...  99.3 us
    unnamed x2, blocking collectives  80.6 us
    all_gather x1, blocking collectives, per_device(): lax.all_gather(down_layout, ('dp', 'fsdp'), axis=0, tiled=True)  43.5 us
    unnamed x11, waiting for transfers between devices  43.4 us
    all_gather x1, blocking collectives, per_device(): lax.all_gather(attn_layout, ('dp', 'fsdp'), axis=1, tiled=True)  43.2 us
  transfers between devices with their start and end apart: 9, of which 5 were waited for; matrix products, arithmetic and copies ran while one was open for 19% of the time, Pallas kernels for 0%

commit v1 on v0

v1 whole, which is shorter than its diff:
```python
import functools

import jax
import jax.numpy as jnp
from jax import lax
from jax.experimental import pallas as pl
from jax.experimental.pallas import tpu as pltpu
from jax.sharding import PartitionSpec as P

HEADS = 12
EPSILON = 1e-05
NEG_FILL = -1000000000.0
AXES = ("dp", "fsdp")
BF16 = jnp.bfloat16
F32 = jnp.float32
ROW_STEP = 64


def mm(a, b, dim_a, dim_b):
    return lax.dot_general(a, b, (((dim_a,), (dim_b,)), ((), ())), preferred_element_type=F32)


def loop(count, body):
    def step(i, carry):
        body(i)
        return carry

    lax.fori_loop(0, count, step, 0)


def steps(total, size):
    size = min(size, total)
    assert total % size == 0
    return total // size, size


def at(i, size):
    return pl.ds(pl.multiple_of(i * size, size), size)


def project_heads(x, weight, qkv, scale, chunk):
    width = x.shape[1]
    count, size = steps(width, chunk)

    def body(i):
        block = mm(weight[at(i, size), :], x[...], 1, 1).astype(BF16).astype(F32)
        qkv[at(i, size), :] = (block * jnp.where(i < count, scale, 1.0)).astype(BF16)

    loop(3 * count, body)


def head_rows(ref, part, head, dim, width):
    return ref[pl.ds(pl.multiple_of(part * width + head * dim, dim), dim), :]


def joined(text_ref, layout_ref, part, head, dims, widths):
    return jnp.concatenate(
        [
            head_rows(text_ref, part, head, dims[0], widths[0]),
            head_rows(layout_ref, part, head, dims[1], widths[1]),
        ],
        axis=0,
    )


def masked_scores(query, key, length):
    scores = mm(key, query, 0, 0)
    place = lax.broadcasted_iota(jnp.int32, scores.shape, 0)
    return jnp.where(place < length, scores, NEG_FILL)


def attend_head(head, length, qkv_t, qkv_l, ctx_t, ctx_l, lse, dims, widths):
    query = joined(qkv_t, qkv_l, 0, head, dims, widths)
    key = joined(qkv_t, qkv_l, 1, head, dims, widths)
    value = joined(qkv_t, qkv_l, 2, head, dims, widths)
    scores = masked_scores(query, key, length)
    top = jnp.max(scores, axis=0, keepdims=True)
    grown = jnp.exp(scores - top)
    total = jnp.sum(grown, axis=0, keepdims=True)
    lse[head] = top + jnp.log(total)
    context = mm(value, grown.astype(BF16), 1, 0) * (1.0 / total)
    ctx_t[pl.ds(pl.multiple_of(head * dims[0], dims[0]), dims[0]), :] = context[: dims[0]].astype(BF16)
    ctx_l[pl.ds(pl.multiple_of(head * dims[1], dims[1]), dims[1]), :] = context[dims[0] :].astype(BF16)


def attend_head_back(
    head, length, qkv_t, qkv_l, dctx_t, dctx_l, lse, dqkv_t, dqkv_l, dims, widths, scales
):
    query = joined(qkv_t, qkv_l, 0, head, dims, widths)
    key = joined(qkv_t, qkv_l, 1, head, dims, widths)
    value = joined(qkv_t, qkv_l, 2, head, dims, widths)
    dcontext = joined(dctx_t, dctx_l, 0, head, dims, widths)
    scores = masked_scores(query, key, length)
    probs = jnp.exp(scores - lse[head])
    dvalue = mm(dcontext, probs.astype(BF16), 1, 1)
    dprobs = mm(value, dcontext, 0, 0)
    inner = jnp.sum(dprobs * probs, axis=0, keepdims=True)
    dscores = (probs * (dprobs - inner)).astype(BF16)
    dkey = mm(query, dscores, 1, 1)
    dquery = mm(key, dscores, 1, 0)
    for part, grad in ((0, dquery), (1, dkey), (2, dvalue)):
        for ref, dim, width, scale, rows in (
            (dqkv_t, dims[0], widths[0], scales[0], grad[: dims[0]]),
            (dqkv_l, dims[1], widths[1], scales[1], grad[dims[0] :]),
        ):
            rows = rows * scale if part == 0 else rows
            ref[pl.ds(pl.multiple_of(part * width + head * dim, dim), dim), :] = rows.astype(BF16)


def normed(hidden):
    centred = hidden - jnp.mean(hidden, axis=-1, keepdims=True)
    rate = lax.rsqrt(jnp.mean(centred * centred, axis=-1, keepdims=True) + EPSILON)
    return centred * rate, rate


def norm_back(grad, hat, rate, gain):
    scaled = grad * gain
    mean = jnp.mean(scaled, axis=-1, keepdims=True)
    along = jnp.mean(scaled * hat, axis=-1, keepdims=True)
    return rate * (scaled - mean - hat * along)


def column_sum(values):
    return jnp.sum(values, axis=0, keepdims=True)


def stream_first(x, ctx_tr, ctx, weight, norms, acc, hat, rate, low):
    rows, width = x.shape
    ctx[...] = ctx_tr[...].T
    count, size = steps(rows, 256)

    def product(i):
        acc[at(i, size), :] = mm(ctx[at(i, size), :], weight[3 * width : 4 * width, :], 1, 1)

    loop(count, product)

    def norm(i):
        block = at(i, ROW_STEP)
        hat_b, rate_b = normed(x[block, :].astype(F32) + acc[block, :])
        hat[block, :] = hat_b
        rate[block, :] = rate_b
        low[block, :] = (hat_b * norms[0:1, :] + norms[1:2, :]).astype(BF16)

    loop(rows // ROW_STEP, norm)


def stream_inner(low, up, down, act, slope, acc, chunk):
    count, size = steps(up.shape[0], chunk)
    acc[...] = jnp.zeros_like(acc)

    def body(i):
        block = at(i, size)
        inner = mm(up[block, :], low[...], 1, 1)
        cdf = 0.5 + 0.5 * lax.erf(inner * (0.5**0.5))
        density = jnp.exp(inner * inner * -0.5) * (0.5 / jnp.pi) ** 0.5
        act[block, :] = (inner * cdf).astype(BF16)
        slope[block, :] = (cdf + inner * density).astype(BF16)
        acc[...] += mm(act[block, :], down[block, :], 0, 0)

    loop(count, body)


def stream_second(g, norms, acc, hat, out, dhid, dlow, gnorm):
    rows, width = g.shape

    def body(i, sums):
        block = at(i, ROW_STEP)
        hidden = hat[block, :] * norms[0:1, :] + norms[1:2, :] + acc[block, :]
        hat_b, rate_b = normed(hidden)
        out[block, :] = (hat_b * norms[2:3, :] + norms[3:4, :]).astype(BF16)
        grad = g[block, :].astype(F32)
        back = norm_back(grad, hat_b, rate_b, norms[2:3, :])
        dhid[block, :] = back
        dlow[block, :] = back.astype(BF16)
        return sums[0] + column_sum(grad * hat_b), sums[1] + column_sum(grad)

    zero = jnp.zeros((1, width), F32)
    sums = lax.fori_loop(0, rows // ROW_STEP, body, (zero, zero))
    gnorm[2:3, :] = sums[0]
    gnorm[3:4, :] = sums[1]


def stream_inner_back(low, dlow, up, down, act, slope, dhid, gup, gdown, chunk, done):
    count, size = steps(up.shape[0], chunk)

    def body(i):
        block = at(i, size)
        dact = mm(down[block, :], dlow[...], 1, 1)
        dinner = (dact * slope[block, :].astype(F32)).astype(BF16)
        dhid[...] += mm(dinner, up[block, :], 0, 0)
        gdown[block, :] = mm(act[block, :], dlow[...], 1, 0).astype(gdown.dtype)
        gup[block, :] = mm(dinner, low[...], 1, 0).astype(gup.dtype)
        done(i, block)

    loop(count, body)
    return count


def stream_first_back(norms, hat, rate, dhid, dlow, ctx, weight, dctx, gattn, gnorm):
    rows, width = hat.shape

    def body(i, sums):
        block = at(i, ROW_STEP)
        grad = dhid[block, :]
        hat_b = hat[block, :]
        back = norm_back(grad, hat_b, rate[block, :], norms[0:1, :])
        dhid[block, :] = back
        dlow[block, :] = back.astype(BF16)
        return sums[0] + column_sum(grad * hat_b), sums[1] + column_sum(grad)

    zero = jnp.zeros((1, width), F32)
    sums = lax.fori_loop(0, rows // ROW_STEP, body, (zero, zero))
    gnorm[0:1, :] = sums[0]
    gnorm[1:2, :] = sums[1]
    dctx[...] = mm(dlow[...], weight[3 * width : 4 * width, :], 1, 0).astype(BF16).T
    gattn[3 * width : 4 * width, :] = mm(dlow[...], ctx[...], 0, 0).astype(gattn.dtype)


def project_back(x, weight, dqkv, dhid, dx, gattn, chunk, done):
    width = x.shape[1]
    count, size = steps(3 * width, chunk)

    def body(i):
        block = at(i, size)
        dhid[...] += mm(dqkv[block, :], weight[block, :], 0, 0)
        gattn[block, :] = mm(dqkv[block, :], x[...], 1, 0).astype(gattn.dtype)
        done(i, block)

    loop(count, body)
    loop(x.shape[0] // ROW_STEP, lambda i: store_low(dx, dhid, at(i, ROW_STEP)))
    return count


def store_low(out, values, block):
    out[block, :] = values[block, :].astype(BF16)


def layer_kernel(dims, scales, chunks, *refs):
    (
        lengths, x, y, gx, gy, tnorm, lnorm, hattn, hup, hdown, lattn, lup, ldown,
        text_out, layout_out, dx, dy, oattn, oup, odown, glattn, glup, gldown, gtnorm, glnorm,
        attn, up, down, qkv_t, qkv_l, dqkv_t, dqkv_l, ctx_tt, ctx_tl, ctx_t, ctx_l, dctx_t, dctx_l,
        act_t, act_l, slope_t, slope_l, acc_t, acc_l, hat_t, hat_l, dhid_t, dhid_l,
        low_t, low_l, dlow_t, dlow_l, rate_t, rate_l, lse, in_sem, out_sem,
    ) = refs
    widths = (x.shape[1], y.shape[1])
    length = lengths[0]
    loads = [
        pltpu.make_async_copy(src, dst, in_sem.at[i])
        for i, (src, dst) in enumerate(((hattn, attn), (hup, up), (hdown, down)))
    ]
    for load in loads:
        load.start()
    project_heads(y, lattn, qkv_l, scales[1], chunks[1])
    loads[0].wait()
    project_heads(x, attn, qkv_t, scales[0], chunks[0])
    loop(
        HEADS,
        lambda h: attend_head(h, length, qkv_t, qkv_l, ctx_tt, ctx_tl, lse, dims, widths),
    )
    loads[1].wait()
    loads[2].wait()
    nothing = lambda i, block: None
    stream_first(y, ctx_tl, ctx_l, lattn, lnorm, acc_l, hat_l, rate_l, low_l)
    stream_inner(low_l, lup, ldown, act_l, slope_l, acc_l, chunks[1])
    stream_second(gy, lnorm, acc_l, hat_l, layout_out, dhid_l, dlow_l, glnorm)
    stream_inner_back(
        low_l, dlow_l, lup, ldown, act_l, slope_l, dhid_l, glup, gldown, chunks[1], nothing
    )
    stream_first_back(lnorm, hat_l, rate_l, dhid_l, dlow_l, ctx_l, lattn, dctx_l, glattn, glnorm)

    def send(source, target, block):
        pltpu.make_async_copy(source.at[block, :], target.at[block, :], out_sem).start()

    def sent_inner(i, block):
        send(up, oup, block)
        send(down, odown, block)

    stream_first(x, ctx_tt, ctx_t, attn, tnorm, acc_t, hat_t, rate_t, low_t)
    stream_inner(low_t, up, down, act_t, slope_t, acc_t, chunks[0])
    stream_second(gx, tnorm, acc_t, hat_t, text_out, dhid_t, dlow_t, gtnorm)
    stream_inner_back(
        low_t, dlow_t, up, down, act_t, slope_t, dhid_t, up, down, chunks[0], sent_inner
    )
    stream_first_back(tnorm, hat_t, rate_t, dhid_t, dlow_t, ctx_t, attn, dctx_t, attn, gtnorm)
    loop(
        HEADS,
        lambda h: attend_head_back(
            h, length, qkv_t, qkv_l, dctx_t, dctx_l, lse, dqkv_t, dqkv_l, dims, widths, scales
        ),
    )
    project_back(y, lattn, dqkv_l, dhid_l, dy, glattn, chunks[1], nothing)
    width = widths[0]
    send(attn, oattn, pl.ds(3 * width, width))
    project_back(
        x, attn, dqkv_t, dhid_t, dx, attn, chunks[0], lambda i, block: send(attn, oattn, block)
    )
    for source, target in ((up, oup), (down, odown), (attn, oattn)):
        pltpu.make_async_copy(source, target, out_sem).wait()


def layer(x, y, lengths, gx, gy, tnorm, lnorm, attn, up, down, lattn, lup, ldown):
    rows, width = x.shape
    lwidth = y.shape[1]
    inner, linner = up.shape[0], lup.shape[0]
    dims = (width // HEADS, lwidth // HEADS)
    scales = tuple(float(dim) ** -0.5 for dim in dims)
    vmem = pl.BlockSpec(memory_space=pltpu.VMEM)
    anywhere = pl.BlockSpec(memory_space=pl.ANY)
    smem = pl.BlockSpec(memory_space=pltpu.SMEM)
    like = jax.ShapeDtypeStruct

    def both(shape_of, dtype):
        return [pltpu.VMEM(shape_of(width, inner), dtype), pltpu.VMEM(shape_of(lwidth, linner), dtype)]

    scratch = [
        pltpu.VMEM(attn.shape, BF16),
        pltpu.VMEM(up.shape, BF16),
        pltpu.VMEM(down.shape, BF16),
        *both(lambda w, f: (3 * w, rows), BF16),
        *both(lambda w, f: (3 * w, rows), BF16),
        *both(lambda w, f: (w, rows), BF16),
        *both(lambda w, f: (rows, w), BF16),
        *both(lambda w, f: (w, rows), BF16),
        *both(lambda w, f: (f, rows), BF16),
        *both(lambda w, f: (f, rows), BF16),
        *both(lambda w, f: (rows, w), F32),
        *both(lambda w, f: (rows, w), F32),
        *both(lambda w, f: (rows, w), F32),
        *both(lambda w, f: (rows, w), BF16),
        *both(lambda w, f: (rows, w), BF16),
        *both(lambda w, f: (rows, 1), F32),
        pltpu.VMEM((HEADS, 1, rows), F32),
        pltpu.SemaphoreType.DMA((3,)),
        pltpu.SemaphoreType.DMA,
    ]
    return pl.pallas_call(
        functools.partial(layer_kernel, dims, scales, (384, 192)),
        out_shape=[
            like(x.shape, BF16),
            like(y.shape, BF16),
            like(x.shape, BF16),
            like(y.shape, BF16),
            like(attn.shape, BF16),
            like(up.shape, BF16),
            like(down.shape, BF16),
            like(lattn.shape, F32),
            like(lup.shape, F32),
            like(ldown.shape, F32),
            like(tnorm.shape, F32),
            like(lnorm.shape, F32),
        ],
        in_specs=[smem] + [vmem] * 6 + [anywhere] * 3 + [vmem] * 3,
        out_specs=[vmem] * 4 + [anywhere] * 3 + [vmem] * 5,
        scratch_shapes=scratch,
        compiler_params=pltpu.CompilerParams(vmem_limit_bytes=67043328),
        name="layer",
    )(lengths, x, y, gx, gy, tnorm, lnorm, attn, up, down, lattn, lup, ldown)


def per_device(
    text_in, layout_in, lengths, attn_text, up_text, down_text,
    attn_layout, up_layout, down_layout, norm_params, grad_text, grad_layout,
):
    width, lwidth = text_in.shape[1], layout_in.shape[1]
    owners = lax.axis_size(AXES)
    part = down_layout.shape[0]
    count = norm_params.shape[0]

    def gather(piece):
        return lax.all_gather(piece, AXES, axis=0, tiled=True)

    attn, up, down = gather(attn_text.T), gather(up_text.T), gather(down_text)
    norm_row = jnp.pad(norm_params, (0, -count % lwidth)).reshape(-1, lwidth)
    small = gather(jnp.concatenate([attn_layout.T, up_layout.T, down_layout, norm_row], axis=0))
    nrows = norm_row.shape[0]
    small = small.reshape(owners, 3 * part + nrows, lwidth)
    lattn, lup, ldown = (
        small[:, i * part : (i + 1) * part].reshape(owners * part, lwidth) for i in range(3)
    )
    norms = small[:, 3 * part :].reshape(owners, -1)[:, :count].reshape(-1).astype(F32)
    tnorm = norms[: 4 * width].reshape(4, width)
    lnorm = norms[4 * width :].reshape(4, lwidth)
    (
        text_out, layout_out, dx, dy, gattn, gup, gdown, glattn, glup, gldown, gtnorm, glnorm,
    ) = layer(
        text_in, layout_in, lengths, grad_text, grad_layout, tnorm, lnorm,
        attn, up, down, lattn, lup, ldown,
    )

    def scatter(piece):
        return lax.psum_scatter(piece, AXES, scatter_dimension=0, tiled=True)

    gnorm = jnp.concatenate([gtnorm.reshape(-1), glnorm.reshape(-1)]).reshape(owners, count)
    gsmall = jnp.concatenate(
        [piece.reshape(owners, part, lwidth) for piece in (glattn, glup, gldown)]
        + [jnp.pad(gnorm, ((0, 0), (0, -count % lwidth))).reshape(owners, nrows, lwidth)],
        axis=1,
    )
    gsmall = scatter(gsmall.reshape(-1, lwidth))
    gattn, gup, gdown = (scatter(piece).astype(F32) for piece in (gattn, gup, gdown))
    return (
        text_out,
        layout_out,
        dx,
        dy,
        gattn.T,
        gup.T,
        gdown,
        gsmall[:part].T,
        gsmall[part : 2 * part].T,
        gsmall[2 * part : 3 * part],
        gsmall[3 * part :].reshape(-1)[:count],
    )


def solution(mesh):
    rows, columns = P(AXES, None), P(None, AXES)
    split = P(AXES)
    return jax.shard_map(
        per_device,
        mesh=mesh,
        in_specs=(
            rows, rows, split, columns, columns, rows, columns, columns, rows, split, rows, rows,
        ),
        out_specs=(rows, rows, rows, rows, columns, columns, rows, columns, columns, rows, split),
        check_vma=False,
    )
```

time: 1110 us -> 776 us (0.70)
  matrix products: 244 us -> 0 us
  blocking collectives: 210 us -> 52.9 us
  Pallas kernels: 0 us -> 82.1 us
  waiting for transfers between devices: 568 us -> 605 us
  local copies, waits for them, and re-layouts: 39.4 us -> 12.2 us
  other arithmetic: 27.1 us -> 8.75 us
    dot_general x36 -> x0, matrix products: 244 us -> none  [the longest x1 30 us: backward_slot(): jnp.einsum('hqk,khd->qhd', text_score_grad, key_text, preferred_element_t...]
    reduce_scatter x4 -> x3, waiting for transfers between devices: 525 us -> 331 us  [scatter(): return lax.psum_scatter(piece, AXES, scatter_dimension=0, tiled=True)]
    all_gather x3, waiting for transfers between devices: 0.02 us -> 140 us  [gather(): return lax.all_gather(piece, AXES, axis=0, tiled=True)]
    unnamed x11 -> x8, waiting for transfers between devices: 43.4 us -> 134 us
    pallas_call x0 -> x1, Pallas kernels: none -> 82.1 us  [layer(): pl.pallas_call(functools.partial(layer_kernel, dims, scales, (384, 192)),...]
    unnamed x2 -> x0, blocking collectives: 80.6 us -> none
    all_gather x3 -> x1, blocking collectives: 129 us -> 52.9 us  [gather(): return lax.all_gather(piece, AXES, axis=0, tiled=True)]
    unnamed x165 -> x11, local copies, waits for them, and re-layouts: 18.7 us -> 4.41 us
  transfers between devices with their start and end apart: 9 -> 7, of which waited for: 5 -> 7; matrix products, arithmetic and copies ran while one was open for 19% -> 2% of each run, Pallas kernels for 0% -> 0%
where the time goes in v1:
time: 776 us
  waiting for transfers between devices  605 us (78%)
  Pallas kernels  82.1 us (11%)
  blocking collectives  52.9 us (7%)
  between operations  14.9 us (2%)
  local copies, waits for them, and re-layouts  12.2 us (2%)
  other arithmetic  8.75 us (1%)
    reduce_scatter x3, waiting for transfers between devices, scatter(): return lax.psum_scatter(piece, AXES, scatter_dimension=0, tiled=True)  331 us
    all_gather x3, waiting for transfers between devices, gather(): return lax.all_gather(piece, AXES, axis=0, tiled=True)  140 us
    unnamed x8, waiting for transfers between devices  134 us
    pallas_call x1, Pallas kernels, layer(): pl.pallas_call(functools.partial(layer_kernel, dims, scales, (384, 192)),...  82.1 us
    all_gather x1, blocking collectives, gather(): return lax.all_gather(piece, AXES, axis=0, tiled=True)  52.9 us
  transfers between devices with their start and end apart: 7, of which 7 were waited for; matrix products, arithmetic and copies ran while one was open for 2% of the time, Pallas kernels for 0%

profile of v1, /device:TPU:0, one launch (start us, length us, event | category | flops | bytes accessed | tf_op | source)
XLA Modules:
  0.0 775.8 jit_solution(4051989289361472225)
XLA Ops:
  10.1 0.8 maximum_bitcast_fusion
  10.9 52.9 %all-gather = bf16[32,73,192]{2,1,0:T(8,128)(2,1)S(1)} all-gather(bf16[1,73,192]{2,1,0:T(8,128)(2,1)S(1)} %maximum_bitcast_fusion), channel_id=1, replica_groups=mesh['dp'=4,'fsdp'=8] {'dp','fsdp'}, dimensions={0}, use_global_device_ids=true | all-gather | bytes 925056 | tf_op jit(solution)/shard_map/all_gather | solution.py:371
  64.0 1.8 copy.39.refs_2_
  65.8 0.8 copy.40.refs_4_
  68.5 1.0 fusion.1
  69.5 9.6 %all-gather.5.cloned.1.call-done.refs_7_ = bf16[3072,768]{1,0:T(8,128)(2,1)} async-done(((bf16[96,768]{1,0:T(8,128)(2,1)}), bf16[3072,768]{1,0:T(8,128)(2,1)}) %all-gather.5.cloned.1.call-update) | async-done | bytes 4718608 | tf_op jit(solution)/shard_map/all_gather | solution.py:371
  79.2 65.0 %all-gather.7.cloned.1.call-done.refs_8_ = bf16[3072,768]{1,0:T(8,128)(2,1)} async-done(((bf16[96,768]{1,0:T(8,128)(2,1)}), bf16[3072,768]{1,0:T(8,128)(2,1)}) %all-gather.7.cloned.1.call-update) | async-done | bytes 4718608 | tf_op jit(solution)/shard_map/all_gather | solution.py:371
  144.1 65.0 %all-gather.9.cloned.1.call-done.refs_9_ = bf16[3072,768]{1,0:T(8,128)(2,1)} async-done(((bf16[96,768]{1,0:T(8,128)(2,1)}), bf16[3072,768]{1,0:T(8,128)(2,1)}) %all-gather.9.cloned.1.call-update) | async-done | bytes 4718608 | tf_op jit(solution)/shard_map/all_gather | solution.py:371
  209.1 82.1 %layer.1 = (bf16[512,768]{1,0:T(8,128)(2,1)}, bf16[512,192]{1,0:T(8,128)(2,1)}, bf16[512,768]{1,0:T(8,128)(2,1)}, bf16[512,192]{1,0:T(8,128)(2,1)}, bf16[3072,76...) custom-call(s32[1]{0:T(128)S(6)} %copy.47.refs_0_, ...), custom_call_target="tpu_custom_call" | custom-call | tf_op jit(solution)/shard_map/layer/pallas_call | solution.py:337
  291.3 0.7 reshape.86
  292.0 0.8 reshape.87
  292.9 1.9 pad_maximum_fusion
  294.8 1.6 reshape.90
  298.5 0.8 copy.41
  299.3 0.8 copy.42
  300.1 130.0 %all-reduce.5.cloned.1.call-done = f32[2336,192]{1,0:T(8,128)} async-done(((f32[2336,192]{1,0:T(8,128)}), f32[2336,192]{1,0:T(8,128)}) %all-reduce.5.cloned.1.call-update) | async-done | bytes 1794064
  430.1 1.2 fusion
  431.3 1.5 constant_dynamic-slice_fusion
  432.8 110.2 %reduce-scatter.6.cloned.1.call-done = bf16[96,768]{1,0:T(8,128)(2,1)} async-done(((bf16[3072,768]{1,0:T(8,128)(2,1)}), bf16[96,768]{1,0:T(8,128)(2,1)}) %reduce-scatter.6.cloned.1.call-update) | async-done | bytes 147472 | tf_op jit(solution)/shard_map/reduce_scatter | solution.py:392
  542.9 1.6 convert_bitcast_fusion
  544.6 110.3 %reduce-scatter.4.cloned.1.call-done = bf16[96,768]{1,0:T(8,128)(2,1)} async-done(((bf16[3072,768]{1,0:T(8,128)(2,1)}), bf16[96,768]{1,0:T(8,128)(2,1)}) %reduce-scatter.4.cloned.1.call-update) | async-done | bytes 147472 | tf_op jit(solution)/shard_map/reduce_scatter | solution.py:392
  654.8 1.6 convert_bitcast_fusion.1
  656.5 110.8 %reduce-scatter.8.cloned.1.call-done = bf16[96,768]{1,0:T(8,128)(2,1)} async-done(((bf16[3072,768]{1,0:T(8,128)(2,1)}), bf16[96,768]{1,0:T(8,128)(2,1)}) %reduce-scatter.8.cloned.1.call-update) | async-done | bytes 147472 | tf_op jit(solution)/shard_map/reduce_scatter | solution.py:392
  767.3 1.6 convert_element_type.20
  (33 shorter events, 6.5 us)
Async XLA Ops:
  7.2 58.6 %copy-start.2 = (bf16[512,192]{0,1:T(8,128)(2,1)S(1)}, bf16[512,192]{0,1:T(8,128)(2,1)}, u32[]{:S(2)}) copy-start(bf16[512,192]{0,1:T(8,128)(2,1)} %param.23) | copy-start | bytes 589828
  7.2 72.0 %all-gather.5.cloned.1.call-start = ((), (), s32[]{:S(2)}) async-start(), calls=%async_computation.3 | async-start | bytes 4866048 | tf_op jit(solution)/shard_map/all_gather | solution.py:371
  7.9 136.2 %all-gather.7.cloned.1.call-start = ((), (), s32[]{:S(2)}) async-start(), calls=%async_computation.4 | async-start | bytes 4866048 | tf_op jit(solution)/shard_map/all_gather | solution.py:371
  8.7 200.5 %all-gather.9.cloned.1.call-start = ((), (), s32[]{:S(2)}) async-start(), calls=%async_computation.5 | async-start | bytes 4866048 | tf_op jit(solution)/shard_map/all_gather | solution.py:371
  9.4 420.7 %all-reduce.5.cloned.1.call-start = ((), (), s32[]{:S(2)}) async-start(), calls=%async_computation.9 | async-start | bytes 4784128
  296.4 246.5 %reduce-scatter.6.cloned.1.call-start = ((), (), s32[]{:S(2)}) async-start(), calls=%async_computation.7 | async-start | bytes 4866048 | tf_op jit(solution)/shard_map/reduce_scatter | solution.py:392
  297.0 357.8 %reduce-scatter.4.cloned.1.call-start = ((), (), s32[]{:S(2)}) async-start(), calls=%async_computation.6 | async-start | bytes 4866048 | tf_op jit(solution)/shard_map/reduce_scatter | solution.py:392
  297.6 1.0 copy-start.1
  297.6 1.7 copy-start
  297.6 469.7 %reduce-scatter.8.cloned.1.call-start = ((), (), s32[]{:S(2)}) async-start(), calls=%async_computation.8 | async-start | bytes 4866048 | tf_op jit(solution)/shard_map/reduce_scatter | solution.py:392
Sparse Core Ops, SparseCore 0:
  11.0 68.1 all-gather.4
  82.2 61.9 all-gather.6
  147.2 61.9 all-gather.8
  296.5 133.5 all-reduce.4
  435.4 107.4 reduce-scatter.5
  548.3 106.5 reduce-scatter.3
  660.3 106.9 reduce-scatter.7

commit v2 on v1

--- a/solution.py
+++ b/solution.py
@@ -358,27 +358,502 @@
     )(lengths, x, y, gx, gy, tnorm, lnorm, attn, up, down, lattn, lup, ldown)
 
 
+def coordinates(planes):
+    pair, column = lax.axis_index("dp"), lax.axis_index("fsdp")
+    x, y = lax.rem(pair, 2), pair // 2
+    plane, core = column // 2, lax.rem(column, 2)
+    across = (pair + 1 - 2 * x, pair + 2 - 4 * y)
+    return pair, plane, core, across
+
+
+def entry_barrier(planes):
+    pair, plane, core, across = coordinates(planes)
+    barrier = pltpu.get_barrier_semaphore()
+
+    def greet(target_pair, target_plane, target_core):
+        pl.semaphore_signal(
+            barrier,
+            inc=1,
+            device_id=(target_pair, target_plane * 2 + target_core),
+            device_id_type=pl.DeviceIdType.MESH,
+        )
+
+    greet(across[0], plane, core)
+    greet(across[1], plane, core)
+    greet(pair, plane, 1 - core)
+    pl.when(plane > 0)(lambda: greet(pair, plane - 1, core))
+    pl.when(plane < planes - 1)(lambda: greet(pair, plane + 1, core))
+    edges = jnp.where(plane > 0, 1, 0) + jnp.where(plane < planes - 1, 1, 0)
+    pl.semaphore_wait(barrier, 3 + edges)
+
+
+class Gather:
+    def __init__(self, planes, units, send_sem, recv_sem):
+        self.planes, self.units = planes, units
+        self.send_sem, self.recv_sem = send_sem, recv_sem
+        self.pair, self.plane, self.core, self.across = coordinates(planes)
+
+    def block(self, unit, pair, plane, core):
+        _, whole, before, after, _ = self.units[unit]
+        return whole.at[(*before, pair, plane, core, *after)]
+
+    def copy(self, unit, block, slot, target, own=False):
+        pair, plane, core = block
+        source = self.units[unit][0] if own else self.block(unit, *block)
+        return pltpu.make_async_remote_copy(
+            src_ref=source,
+            dst_ref=self.block(unit, *block),
+            send_sem=self.send_sem.at[unit, slot],
+            recv_sem=self.recv_sem.at[unit, (pair * self.planes + plane) * 2 + core],
+            device_id=(target[0], target[1] * 2 + target[2]),
+            device_id_type=pl.DeviceIdType.MESH,
+        )
+
+    def arrived(self, unit, pair, plane, core):
+        here = (self.pair, self.plane, self.core)
+        self.copy(unit, (pair, plane, core), 0, here).wait_recv()
+
+    def partners(self, unit):
+        order = self.units[unit][4]
+        near, far = self.across[order], self.across[1 - order]
+        both = self.across[0] + self.across[1] - self.pair
+        return near, far, both
+
+    def slot(self, kind, plane):
+        return 2 + kind * self.planes + plane
+
+    def spread(self, unit, pair, plane, own=False):
+        near, far, _ = self.partners(unit)
+        block = (pair, plane, self.core)
+        here = (self.plane, self.core)
+        self.copy(unit, block, self.slot(1, plane), (near, *here), own).start()
+        self.copy(unit, block, self.slot(2, plane), (far, *here), own).start()
+        self.copy(unit, block, self.slot(4, plane), (self.pair, self.plane, 1 - self.core), own).start()
+
+    def launch(self, unit):
+        block = (self.pair, self.plane, self.core)
+        for up in (0, 1):
+            step = 2 * up - 1
+            inside = (self.plane + step >= 0) & (self.plane + step < self.planes)
+            pl.when(inside)(
+                lambda up=up, step=step: self.copy(
+                    unit, block, up, (self.pair, self.plane + step, self.core), True
+                ).start()
+            )
+        self.spread(unit, self.pair, self.plane, True)
+
+    def along(self, unit, distance):
+        for step in (-1, 1):
+            origin = self.plane - step * distance
+            ahead = self.plane + step
+
+            def take(origin=origin, ahead=ahead):
+                self.arrived(unit, self.pair, origin, self.core)
+                pl.when((ahead >= 0) & (ahead < self.planes))(
+                    lambda: self.copy(
+                        unit,
+                        (self.pair, origin, self.core),
+                        self.slot(0, origin),
+                        (self.pair, ahead, self.core),
+                    ).start()
+                )
+                self.spread(unit, self.pair, origin)
+
+            pl.when((origin >= 0) & (origin < self.planes))(take)
+
+    def from_near(self, unit):
+        near, far, _ = self.partners(unit)
+        for plane in range(self.planes):
+            self.arrived(unit, near, plane, self.core)
+            block = (near, plane, self.core)
+            self.copy(unit, block, self.slot(3, plane), (far, self.plane, self.core)).start()
+            self.copy(
+                unit, block, self.slot(5, plane), (self.pair, self.plane, 1 - self.core)
+            ).start()
+
+    def from_far(self, unit):
+        _, far, both = self.partners(unit)
+        for kind, pair in ((6, far), (7, both)):
+            for plane in range(self.planes):
+                self.arrived(unit, pair, plane, self.core)
+                self.copy(
+                    unit,
+                    (pair, plane, self.core),
+                    self.slot(kind, plane),
+                    (self.pair, self.plane, 1 - self.core),
+                ).start()
+
+    def from_core(self, unit):
+        near, far, both = self.partners(unit)
+        for pair in (self.pair, near, far, both):
+            for plane in range(self.planes):
+                self.arrived(unit, pair, plane, 1 - self.core)
+
+    def drain(self, unit):
+        block = (self.pair, self.plane, self.core)
+        here = block
+
+        def sent(slot):
+            self.copy(unit, block, slot, here, True).wait_send()
+
+        for up in (0, 1):
+            step = 2 * up - 1
+            ahead = self.plane + step
+            pl.when((ahead >= 0) & (ahead < self.planes))(lambda up=up: sent(up))
+            for distance in range(1, self.planes):
+                origin = self.plane - step * distance
+                inside = (origin >= 0) & (origin < self.planes)
+                onward = inside & (ahead >= 0) & (ahead < self.planes)
+                pl.when(onward)(lambda origin=origin: sent(self.slot(0, origin)))
+        for kind in range(1, 8):
+            for plane in range(self.planes):
+                sent(self.slot(kind, plane))
+
+    @staticmethod
+    def slots(planes):
+        return 2 + 8 * planes
+
+
+def gather_kernel(planes, own, small, *refs):
+    parts = own.shape[0]
+    wholes, small_whole = refs[:parts], refs[parts]
+    local_sem, send_sem, recv_sem = refs[parts + 1 :]
+    units = []
+    for part in range(parts):
+        units += [(own.at[part, half], wholes[part], (), (half,), half) for half in (0, 1)]
+        if part == 0:
+            units.append((small, small_whole, (), (), 0))
+    entry_barrier(planes)
+    run = Gather(planes, units, send_sem, recv_sem)
+    here = (run.pair, run.plane, run.core)
+    keeps = [
+        pltpu.make_async_copy(source, run.block(unit, *here), local_sem.at[unit])
+        for unit, (source, *_) in enumerate(units)
+    ]
+    for keep in keeps:
+        keep.start()
+    groups = [[0, 1, 2]] + [[3 + 2 * i, 4 + 2 * i] for i in range(parts - 1)]
+
+    def each(step, at_group):
+        if 0 <= at_group < len(groups):
+            for unit in groups[at_group]:
+                step(unit)
+
+    def along(at_group):
+        for distance in range(1, planes):
+            each(lambda unit: run.along(unit, distance), at_group)
+
+    each(run.launch, 0)
+    for at_group in range(len(groups) + 2):
+        along(at_group)
+        each(run.launch, at_group + 1)
+        each(run.from_near, at_group - 1)
+        each(run.from_far, at_group - 2)
+    for unit in range(len(units)):
+        run.from_core(unit)
+    for unit in range(len(units)):
+        run.drain(unit)
+    for keep in keeps:
+        keep.wait()
+
+
+def gather_blocks(own, small, planes):
+    parts, _, half, width = own.shape
+    count = 2 * parts + 1
+    anywhere = pl.BlockSpec(memory_space=pl.ANY)
+    return pl.pallas_call(
+        functools.partial(gather_kernel, planes),
+        out_shape=[
+            *[jax.ShapeDtypeStruct((4, planes, 2, 2, half, width), own.dtype)] * parts,
+            jax.ShapeDtypeStruct((4, planes, 2, *small.shape), small.dtype),
+        ],
+        in_specs=[anywhere] * 2,
+        out_specs=[anywhere] * (parts + 1),
+        scratch_shapes=[
+            pltpu.SemaphoreType.DMA((count,)),
+            pltpu.SemaphoreType.DMA((count, Gather.slots(planes))),
+            pltpu.SemaphoreType.DMA((count, 8 * planes)),
+        ],
+        compiler_params=pltpu.CompilerParams(collective_id=0, has_side_effects=True),
+        name="gather_blocks",
+    )(own, small)
+
+
+class Scatter:
+    def __init__(self, planes, units, send_sem, recv_sem):
+        self.planes, self.units = planes, units
+        self.send_sem, self.recv_sem = send_sem, recv_sem
+        self.pair, self.plane, self.core, self.across = coordinates(planes)
+
+    def partners(self, unit):
+        order = self.units[unit][3]
+        near, far = self.across[order], self.across[1 - order]
+        return near, far, self.across[0] + self.across[1] - self.pair
+
+    def blocks(self, unit, pair, core):
+        whole, before, after = self.units[unit][:3]
+        return whole.at[(*before, pair, slice(None), core, *after)]
+
+    def copy(self, unit, slot, source, target, device):
+        return pltpu.make_async_remote_copy(
+            src_ref=source,
+            dst_ref=target,
+            send_sem=self.send_sem.at[unit, slot],
+            recv_sem=self.recv_sem.at[unit, slot],
+            device_id=(device[0], device[1] * 2 + device[2]),
+            device_id_type=pl.DeviceIdType.MESH,
+        )
+
+    def core_copy(self, unit, pair):
+        held = self.units[unit][4]
+        return self.copy(
+            unit,
+            pair,
+            self.blocks(unit, pair, 1 - self.core),
+            held["core"].at[pair],
+            (self.pair, self.plane, 1 - self.core),
+        )
+
+    def far_copy(self, unit, which, pair):
+        held = self.units[unit][4]
+        _, far, _ = self.partners(unit)
+        return self.copy(
+            unit, 4 + which, held["core"].at[pair], held["far"].at[which], (far, self.plane, self.core)
+        )
+
+    def near_copy(self, unit):
+        held = self.units[unit][4]
+        near, _, _ = self.partners(unit)
+        return self.copy(
+            unit, 6, held["far"].at[1], held["near"], (near, self.plane, self.core)
+        )
+
+    def z_copy(self, unit, up, plane, first):
+        held = self.units[unit][4]
+        source = held["near"].at[plane] if first else held["z"].at[up, plane]
+        step = 2 * up - 1
+        return self.copy(
+            unit,
+            7 + up * self.planes + plane,
+            source,
+            held["z"].at[up, plane],
+            (self.pair, self.plane + step, self.core),
+        )
+
+    def local_copy(self, unit, pair, local_sem):
+        held = self.units[unit][4]
+        return pltpu.make_async_copy(
+            self.blocks(unit, pair, self.core), held["own"].at[pair], local_sem.at[unit, pair]
+        )
+
+    def launch(self, unit, local_sem):
+        near, far, both = self.partners(unit)
+        for pair in (both, far, near, self.pair):
+            self.core_copy(unit, pair).start()
+            self.local_copy(unit, pair, local_sem).start()
+
+    def add(self, target, term):
+        def body(i):
+            total = target[i].astype(F32) + term[i].astype(F32)
+            target[i] = total.astype(target.dtype)
+
+        loop(self.planes, body)
+
+    def from_core(self, unit, local_sem):
+        held = self.units[unit][4]
+        near, far, both = self.partners(unit)
+        for which, pair in ((1, both), (0, far), (None, near), (None, self.pair)):
+            self.core_copy(unit, pair).wait_recv()
+            self.local_copy(unit, pair, local_sem).wait()
+            self.add(held["core"].at[pair], held["own"].at[pair])
+            if which is not None:
+                self.far_copy(unit, which, pair).start()
+
+    def from_far(self, unit):
+        held = self.units[unit][4]
+        near, far, both = self.partners(unit)
+        self.far_copy(unit, 1, both).wait_recv()
+        self.add(held["far"].at[1], held["core"].at[near])
+        self.near_copy(unit).start()
+        self.far_copy(unit, 0, far).wait_recv()
+        self.add(held["far"].at[0], held["core"].at[self.pair])
+
+    def z_cases(self, up):
+        step = 2 * up - 1
+        behind = self.plane - step
+        starts = (behind < 0) | (behind >= self.planes)
+        for distance in range(self.planes - 1, 0, -1):
+            target = self.plane + step * distance
+            inside = (target >= 0) & (target < self.planes)
+            yield target, inside & starts, inside & jnp.logical_not(starts)
+
+    def from_near(self, unit):
+        held = self.units[unit][4]
+        self.near_copy(unit).wait_recv()
+        self.add(held["near"], held["far"].at[0])
+        for up in (0, 1):
+            for target, starts, _ in self.z_cases(up):
+                pl.when(starts)(
+                    lambda up=up, target=target: self.z_copy(unit, up, target, True).start()
+                )
+
+    def from_z(self, unit):
+        held = self.units[unit][4]
+        for cases in zip(self.z_cases(0), self.z_cases(1)):
+            for up, (target, _, passes) in enumerate(cases):
+
+                def go(up=up, target=target):
+                    self.z_copy(unit, up, target, False).wait_recv()
+                    place = held["z"].at[up, target]
+                    total = place[...].astype(F32) + held["near"][target].astype(F32)
+                    place[...] = total.astype(place.dtype)
+                    self.z_copy(unit, up, target, False).start()
+
+                pl.when(passes)(go)
+
+    def finish(self, unit):
+        held, place = self.units[unit][4:]
+        place[...] = held["near"][self.plane].astype(F32)
+        for up in (0, 1):
+            behind = self.plane - (2 * up - 1)
+
+            def take(up=up):
+                self.z_copy(unit, up, self.plane, False).wait_recv()
+                place[...] += held["z"][up, self.plane].astype(F32)
+
+            pl.when((behind >= 0) & (behind < self.planes))(take)
+
+    def drain(self, unit):
+        near, far, both = self.partners(unit)
+        for pair in (both, far, near, self.pair):
+            self.core_copy(unit, pair).wait_send()
+        self.far_copy(unit, 1, both).wait_send()
+        self.far_copy(unit, 0, far).wait_send()
+        self.near_copy(unit).wait_send()
+        for up in (0, 1):
+            for target, starts, passes in self.z_cases(up):
+                pl.when(starts | passes)(
+                    lambda up=up, target=target: self.z_copy(unit, up, target, False).wait_send()
+                )
+
+    @staticmethod
+    def slots(planes):
+        return 7 + 2 * planes
+
+    @staticmethod
+    def buffers(planes, block, dtype):
+        return [
+            pltpu.VMEM((4, planes, *block), dtype),
+            pltpu.VMEM((4, planes, *block), dtype),
+            pltpu.VMEM((2, planes, *block), dtype),
+            pltpu.VMEM((planes, *block), dtype),
+            pltpu.VMEM((2, planes, *block), dtype),
+        ]
+
+
+def named(refs, index=None):
+    names = ("own", "core", "far", "near", "z")
+    return {n: ref if index is None else ref.at[index] for n, ref in zip(names, refs)}
+
+
+def scatter_kernel(planes, count, *refs):
+    wholes, (small_whole,) = refs[:count], refs[count : count + 1]
+    outs, (small_out,) = refs[count + 1 : 2 * count + 1], refs[2 * count + 1 : 2 * count + 2]
+    rest = refs[2 * count + 2 :]
+    local_sem, send_sem, recv_sem = rest[-3:]
+    held = rest[:-3]
+    entry_barrier(planes)
+    units = []
+    for part in range(count):
+        for half in (0, 1):
+            at_unit = 5 * len(units)
+            units.append(
+                (wholes[part], (), (half,), half, named(held[at_unit : at_unit + 5]), outs[part].at[half])
+            )
+    units.append((small_whole, (), (), 0, named(held[-5:]), small_out))
+    run = Scatter(planes, units, send_sem, recv_sem)
+    order = list(range(len(units)))
+    order = order[:2] + [order[-1]] + order[2:-1]
+    stages = (
+        (0, lambda unit: run.launch(unit, local_sem)),
+        (1, lambda unit: run.from_core(unit, local_sem)),
+        (3, run.from_far),
+        (5, run.from_near),
+        (7, run.from_z),
+        (8, run.finish),
+    )
+    for at_step in range(len(order) + stages[-1][0]):
+        for delay, stage in stages:
+            if 0 <= at_step - delay < len(order):
+                stage(order[at_step - delay])
+    for unit in order:
+        run.drain(unit)
+
+
+def scatter_blocks(wholes, small, planes):
+    count = len(wholes)
+    block = wholes[0].shape[-2:]
+    anywhere = pl.BlockSpec(memory_space=pl.ANY)
+    vmem = pl.BlockSpec(memory_space=pltpu.VMEM)
+    units = 2 * count + 1
+    buffers = []
+    for _ in range(2 * count):
+        buffers += Scatter.buffers(planes, block, wholes[0].dtype)
+    buffers += Scatter.buffers(planes, small.shape[-2:], small.dtype)
+    return pl.pallas_call(
+        functools.partial(scatter_kernel, planes, count),
+        out_shape=[jax.ShapeDtypeStruct((2, *block), F32)] * count
+        + [jax.ShapeDtypeStruct(small.shape[-2:], F32)],
+        in_specs=[anywhere] * (count + 1),
+        out_specs=[vmem] * (count + 1),
+        scratch_shapes=[
+            *buffers,
+            pltpu.SemaphoreType.DMA((units, 4)),
+            pltpu.SemaphoreType.DMA((units, Scatter.slots(planes))),
+            pltpu.SemaphoreType.DMA((units, Scatter.slots(planes))),
+        ],
+        compiler_params=pltpu.CompilerParams(
+            collective_id=1, has_side_effects=True, vmem_limit_bytes=67043328
+        ),
+        name="scatter_blocks",
+    )(*wholes, small)
+def pack_small(pieces, norm_part, multiple):
+    owners, _, width = pieces[0].shape
+    norm_rows = jnp.pad(norm_part, ((0, 0), (0, -norm_part.shape[1] % width)))
+    block = jnp.concatenate([*pieces, norm_rows.reshape(owners, -1, width)], axis=1)
+    return jnp.pad(block, ((0, 0), (0, -block.shape[1] % multiple), (0, 0)))
+
+
+def unpack_small(block, part, count):
+    pieces = [block[:, i * part : (i + 1) * part] for i in range(3)]
+    return pieces, block[:, 3 * part :].reshape(block.shape[0], -1)[:, :count]
+
+
 def per_device(
-    text_in, layout_in, lengths, attn_text, up_text, down_text,
+    planes, text_in, layout_in, lengths, attn_text, up_text, down_text,
     attn_layout, up_layout, down_layout, norm_params, grad_text, grad_layout,
 ):
     width, lwidth = text_in.shape[1], layout_in.shape[1]
     owners = lax.axis_size(AXES)
-    part = down_layout.shape[0]
+    text_part, part = down_text.shape[0], down_layout.shape[0]
     count = norm_params.shape[0]
-
-    def gather(piece):
-        return lax.all_gather(piece, AXES, axis=0, tiled=True)
-
-    attn, up, down = gather(attn_text.T), gather(up_text.T), gather(down_text)
-    norm_row = jnp.pad(norm_params, (0, -count % lwidth)).reshape(-1, lwidth)
-    small = gather(jnp.concatenate([attn_layout.T, up_layout.T, down_layout, norm_row], axis=0))
-    nrows = norm_row.shape[0]
-    small = small.reshape(owners, 3 * part + nrows, lwidth)
-    lattn, lup, ldown = (
-        small[:, i * part : (i + 1) * part].reshape(owners * part, lwidth) for i in range(3)
-    )
-    norms = small[:, 3 * part :].reshape(owners, -1)[:, :count].reshape(-1).astype(F32)
+    own_text = [attn_text.T, up_text.T, down_text]
+    own_small = pack_small(
+        [attn_layout.T[None], up_layout.T[None], down_layout[None]], norm_params[None], 16
+    )[0]
+    if planes:
+        half = text_part // 2
+        own = jnp.stack(own_text).reshape(3, 2, half, width)
+        *wholes, small = gather_blocks(own, own_small, planes)
+        attn, up, down = (whole.reshape(owners * text_part, width) for whole in wholes)
+        small = small.reshape(owners, *own_small.shape)
+    else:
+        gather = lambda piece: lax.all_gather(piece, AXES, axis=0, tiled=True)
+        attn, up, down = (gather(piece) for piece in own_text)
+        small = gather(own_small[None])
+    pieces, norms = unpack_small(small, part, count)
+    lattn, lup, ldown = (piece.reshape(owners * part, lwidth) for piece in pieces)
+    norms = norms.reshape(-1).astype(F32)
     tnorm = norms[: 4 * width].reshape(4, width)
     lnorm = norms[4 * width :].reshape(4, lwidth)
     (
@@ -387,38 +862,38 @@
         text_in, layout_in, lengths, grad_text, grad_layout, tnorm, lnorm,
         attn, up, down, lattn, lup, ldown,
     )
-
-    def scatter(piece):
-        return lax.psum_scatter(piece, AXES, scatter_dimension=0, tiled=True)
-
     gnorm = jnp.concatenate([gtnorm.reshape(-1), glnorm.reshape(-1)]).reshape(owners, count)
-    gsmall = jnp.concatenate(
-        [piece.reshape(owners, part, lwidth) for piece in (glattn, glup, gldown)]
-        + [jnp.pad(gnorm, ((0, 0), (0, -count % lwidth))).reshape(owners, nrows, lwidth)],
-        axis=1,
+    gsmall = pack_small(
+        [piece.reshape(owners, part, lwidth) for piece in (glattn, glup, gldown)], gnorm, 16
+    ).astype(BF16)
+    if planes:
+        shape = (4, planes, 2, 2, text_part // 2, width)
+        gattn, gup, gdown, gsmall = scatter_blocks(
+            [grad.reshape(shape) for grad in (gattn, gup, gdown)],
+            gsmall.reshape(4, planes, 2, *gsmall.shape[1:]),
+            planes,
+        )
+        gattn, gup, gdown = (grad.reshape(text_part, width) for grad in (gattn, gup, gdown))
+    else:
+        scatter = lambda piece: lax.psum_scatter(piece, AXES, scatter_dimension=0, tiled=True)
+        gattn, gup, gdown, gsmall = (
+            scatter(grad).astype(F32) for grad in (gattn, gup, gdown, gsmall)
+        )
+        gsmall = gsmall[0]
+    pieces, gnorm = unpack_small(gsmall[None], part, count)
+    glattn, glup, gldown = (piece[0] for piece in pieces)
+    return (
+        text_out, layout_out, dx, dy, gattn.T, gup.T, gdown, glattn.T, glup.T, gldown, gnorm[0],
     )
-    gsmall = scatter(gsmall.reshape(-1, lwidth))
-    gattn, gup, gdown = (scatter(piece).astype(F32) for piece in (gattn, gup, gdown))
-    return (
-        text_out,
-        layout_out,
-        dx,
-        dy,
-        gattn.T,
-        gup.T,
-        gdown,
-        gsmall[:part].T,
-        gsmall[part : 2 * part].T,
-        gsmall[2 * part : 3 * part],
-        gsmall[3 * part :].reshape(-1)[:count],
-    )
 
 
 def solution(mesh):
+    pairs, columns_on_axis = mesh.shape["dp"], mesh.shape["fsdp"]
+    planes = columns_on_axis // 2 if pairs == 4 and columns_on_axis % 2 == 0 else 0
     rows, columns = P(AXES, None), P(None, AXES)
     split = P(AXES)
     return jax.shard_map(
-        per_device,
+        functools.partial(per_device, planes),
         mesh=mesh,
         in_specs=(
             rows, rows, split, columns, columns, rows, columns, columns, rows, split, rows, rows,

time: 776 us -> 278 us (0.36)
  waiting for transfers between devices: 605 us -> 0 us
  Pallas kernels: 82.1 us -> 248 us
  blocking collectives: 52.9 us -> 0 us
  between operations: 14.9 us -> 1.42 us
    reduce_scatter x3 -> x0, waiting for transfers between devices: 331 us -> none  [scatter(): return lax.psum_scatter(piece, AXES, scatter_dimension=0, tiled=True)]
    pallas_call x0 -> x2, Pallas kernels: none -> 166 us  [the longest x1 89.6 us: scatter_blocks(): pl.pallas_call(functools.partial(scatter_kernel, planes, count), out_shap...]
    all_gather x3 -> x0, waiting for transfers between devices: 140 us -> none  [gather(): return lax.all_gather(piece, AXES, axis=0, tiled=True)]
    unnamed x8 -> x0, waiting for transfers between devices: 134 us -> none
    all_gather x1 -> x0, blocking collectives: 52.9 us -> none  [gather(): return lax.all_gather(piece, AXES, axis=0, tiled=True)]
  transfers between devices with their start and end apart: 7 -> 0, of which waited for: 7 -> 0; matrix products, arithmetic and copies ran while one was open for 2% -> 0% of each run, Pallas kernels for 0% -> 0%
where the time goes in v2:
time: 278 us; the launch traced here: 277 us
  Pallas kernels  248 us (89%)
  local copies, waits for them, and re-layouts  19.3 us (7%)
  other arithmetic  8.54 us (3%)
    pallas_call x1, Pallas kernels, scatter_blocks(): pl.pallas_call(functools.partial(scatter_kernel, planes, count), out_shap...  89.6 us
    pallas_call x1, Pallas kernels, layer(): pl.pallas_call(functools.partial(layer_kernel, dims, scales, (384, 192)),...  82.1 us
    pallas_call x1, Pallas kernels, gather_blocks(): pl.pallas_call(functools.partial(gather_kernel, planes), out_shape=[*[jax...  76.3 us
    unnamed x11, local copies, waits for them, and re-layouts  12.1 us

profile of v2, /device:TPU:0, one launch (start us, length us, event | category | flops | bytes accessed | tf_op | source)
XLA Modules:
  0.0 277.3 jit_solution(9537671534508094017)
XLA Ops:
  1.3 0.7 pad_bitcast_fusion.1
  2.0 1.4 fusion.14.small
  3.3 1.8 copy.27.refs_2_
  5.1 1.8 copy.28.refs_4_
  6.9 1.9 pad_maximum_fusion.own
  8.7 76.3 %gather_blocks.1 = (bf16[4,4,2,2,48,768]{5,4,3,2,1,0:T(8,128)(2,1)}, bf16[4,4,2,2,48,768]{5,4,3,2,1,0:T(8,128)(2,1)}, bf16[4,4,2,2,48,768]{5,4,3,2,1,0:T(8,128)(2,1)}, bf16[4,4,2,80,192]{4,3,2,1,0:T(8,128)(2,1)}) custom-call(bf16[3,2,48,768]{3,2,1,0:T(8,128)(2,1)} %pad_maximum_fusion.own, bf16[80,192]{1,0:T(8,128)(2,1)} %fusion.14.small), custom_call_target="tpu_custom_call" | custom-call | tf_op jit(solution)/shard_map/gather_blocks/pallas_call | solution.py:564
  85.1 0.9 slice.58
  86.0 2.3 fusion.15
  88.6 0.6 slice_convert_fusion.1.refs_6_
  89.3 0.6 slice_convert_fusion.refs_5_
  89.9 82.1 %layer.1 = (bf16[512,768]{1,0:T(8,128)(2,1)}, bf16[512,192]{1,0:T(8,128)(2,1)}, bf16[512,768]{1,0:T(8,128)(2,1)}, bf16[512,192]{1,0:T(8,128)(2,1)}, bf16[3072,76...) custom-call(s32[1]{0:T(128)S(6)} %copy.35.refs_0_, ...), custom_call_target="tpu_custom_call" | custom-call | tf_op jit(solution)/shard_map/layer/pallas_call | solution.py:337
  172.0 0.8 convert.35
  172.9 0.7 convert.34
  173.8 1.8 copy.30
  175.5 1.8 copy.31
  177.3 1.2 convert.31
  178.6 1.3 fusion.6
  179.9 89.6 %scatter_blocks.1 = (f32[2,48,768]{2,1,0:T(8,128)}, f32[2,48,768]{2,1,0:T(8,128)}, f32[2,48,768]{2,1,0:T(8,128)}, f32[80,192]{1,0:T(8,128)}) custom-call(bf16[4,4,2,2,48,768]{5,4,3,2,1,0:T(8,128)(2,1)} %bitcast.56, bf16[4,4,2,2,48,768]{5,4,3,2,1,0:T(8,128)(2,1)} %bitcast.57, bf16[4,4,2,2,48,768]{5,4,3,2,1,0:T(8,128)(2,1)} %bitcast.58, ...), custom_call_target="tpu_custom_call" | custom-call | tf_op jit(solution)/shard_map/scatter_blocks/pallas_call | solution.py:803
  269.5 0.7 slice.68
  270.2 1.4 slice_bitcast_fusion
  271.7 0.5 slice_bitcast_fusion.3
  272.2 1.7 copy.36
  273.9 1.7 copy.37
  275.6 1.7 copy.38
  (17 shorter events, 0.7 us)
Async XLA Ops:
  172.0 6.5 %copy-start.1 = (f32[768,192]{1,0:T(8,128)S(1)}, f32[768,192]{1,0:T(8,128)}, u32[]{:S(2)}) copy-start(f32[768,192]{1,0:T(8,128)} %get-tuple-element.43) | copy-start | bytes 1769476
  172.0 6.5 %copy-start = (f32[768,192]{1,0:T(8,128)S(1)}, f32[768,192]{1,0:T(8,128)}, u32[]{:S(2)}) copy-start(f32[768,192]{1,0:T(8,128)} %get-tuple-element.44) | copy-start | bytes 1769476

commit v3 on v1

--- a/solution.py
+++ b/solution.py
@@ -144,9 +144,8 @@
     loop(rows // ROW_STEP, norm)
 
 
-def stream_inner(low, up, down, act, slope, acc, chunk):
+def stream_up(low, up, act, slope, chunk):
     count, size = steps(up.shape[0], chunk)
-    acc[...] = jnp.zeros_like(acc)
 
     def body(i):
         block = at(i, size)
@@ -155,9 +154,19 @@
         density = jnp.exp(inner * inner * -0.5) * (0.5 / jnp.pi) ** 0.5
         act[block, :] = (inner * cdf).astype(BF16)
         slope[block, :] = (cdf + inner * density).astype(BF16)
+
+    loop(count, body)
+
+
+def stream_down(act, down, acc, chunk):
+    count, size = steps(down.shape[0], chunk)
+    acc[...] = mm(act[:size, :], down[:size, :], 0, 0)
+
+    def body(i):
+        block = at(i + 1, size)
         acc[...] += mm(act[block, :], down[block, :], 0, 0)
 
-    loop(count, body)
+    loop(count - 1, body)
 
 
 def stream_second(g, norms, acc, hat, out, dhid, dlow, gnorm):
@@ -262,7 +271,8 @@
     loads[2].wait()
     nothing = lambda i, block: None
     stream_first(y, ctx_tl, ctx_l, lattn, lnorm, acc_l, hat_l, rate_l, low_l)
-    stream_inner(low_l, lup, ldown, act_l, slope_l, acc_l, chunks[1])
+    stream_up(low_l, lup, act_l, slope_l, chunks[1])
+    stream_down(act_l, ldown, acc_l, chunks[1])
     stream_second(gy, lnorm, acc_l, hat_l, layout_out, dhid_l, dlow_l, glnorm)
     stream_inner_back(
         low_l, dlow_l, lup, ldown, act_l, slope_l, dhid_l, glup, gldown, chunks[1], nothing
@@ -277,7 +287,8 @@
         send(down, odown, block)
 
     stream_first(x, ctx_tt, ctx_t, attn, tnorm, acc_t, hat_t, rate_t, low_t)
-    stream_inner(low_t, up, down, act_t, slope_t, acc_t, chunks[0])
+    stream_up(low_t, up, act_t, slope_t, chunks[0])
+    stream_down(act_t, down, acc_t, chunks[0])
     stream_second(gx, tnorm, acc_t, hat_t, text_out, dhid_t, dlow_t, gtnorm)
     stream_inner_back(
         low_t, dlow_t, up, down, act_t, slope_t, dhid_t, up, down, chunks[0], sent_inner
@@ -358,67 +369,686 @@
     )(lengths, x, y, gx, gy, tnorm, lnorm, attn, up, down, lattn, lup, ldown)
 
 
-def per_device(
+def coordinates(planes):
+    pair, column = lax.axis_index("dp"), lax.axis_index("fsdp")
+    x, y = lax.rem(pair, 2), pair // 2
+    plane, core = column // 2, lax.rem(column, 2)
+    across = (pair + 1 - 2 * x, pair + 2 - 4 * y)
+    return pair, plane, core, across
+
+
+def entry_barrier(planes):
+    pair, plane, core, across = coordinates(planes)
+    barrier = pltpu.get_barrier_semaphore()
+
+    def greet(target_pair, target_plane, target_core):
+        pl.semaphore_signal(
+            barrier,
+            inc=1,
+            device_id=(target_pair, target_plane * 2 + target_core),
+            device_id_type=pl.DeviceIdType.MESH,
+        )
+
+    greet(across[0], plane, core)
+    greet(across[1], plane, core)
+    greet(pair, plane, 1 - core)
+    pl.when(plane > 0)(lambda: greet(pair, plane - 1, core))
+    pl.when(plane < planes - 1)(lambda: greet(pair, plane + 1, core))
+    edges = jnp.where(plane > 0, 1, 0) + jnp.where(plane < planes - 1, 1, 0)
+    pl.semaphore_wait(barrier, 3 + edges)
+
+
+class Route:
+    def __init__(self, planes, units, send_sem, recv_sem):
+        self.planes, self.units = planes, units
+        self.send_sem, self.recv_sem = send_sem, recv_sem
+        self.pair, self.plane, self.core, self.across = coordinates(planes)
+
+    def partners(self, unit):
+        order = self.units[unit]["order"]
+        near, far = self.across[order], self.across[1 - order]
+        return near, far, self.across[0] + self.across[1] - self.pair
+
+    def inside(self, plane):
+        return (plane >= 0) & (plane < self.planes)
+
+    def remote(self, source, target, unit, send_slot, recv_slot, device):
+        return pltpu.make_async_remote_copy(
+            src_ref=source,
+            dst_ref=target,
+            send_sem=self.send_sem.at[unit, send_slot],
+            recv_sem=self.recv_sem.at[unit, recv_slot],
+            device_id=(device[0], device[1] * 2 + device[2]),
+            device_id_type=pl.DeviceIdType.MESH,
+        )
+
+
+class Gather(Route):
+    def copy(self, unit, block, slot, target, own=False):
+        pair, plane, core = block
+        place = self.units[unit]["place"](*block)
+        source = self.units[unit]["own"] if own else place
+        arrival = (pair * self.planes + plane) * 2 + core
+        return self.remote(source, place, unit, slot, arrival, target)
+
+    def arrived(self, unit, pair, plane, core):
+        here = (self.pair, self.plane, self.core)
+        self.copy(unit, (pair, plane, core), 0, here).wait_recv()
+
+    def slot(self, kind, plane):
+        return 2 + kind * self.planes + plane
+
+    @staticmethod
+    def slots(planes):
+        return 2 + 8 * planes
+
+    def spread(self, unit, plane, own=False):
+        near, far, _ = self.partners(unit)
+        block = (self.pair, plane, self.core)
+        for kind, pair, core in ((1, near, self.core), (2, far, self.core), (4, self.pair, 1 - self.core)):
+            self.copy(unit, block, self.slot(kind, plane), (pair, self.plane, core), own).start()
+
+    def launch(self, unit):
+        block = (self.pair, self.plane, self.core)
+        for up in (0, 1):
+            ahead = self.plane + 2 * up - 1
+            pl.when(self.inside(ahead))(
+                lambda up=up, ahead=ahead: self.copy(
+                    unit, block, up, (self.pair, ahead, self.core), True
+                ).start()
+            )
+        self.spread(unit, self.plane, True)
+
+    def along(self, unit, distance):
+        for step in (-1, 1):
+            origin, ahead = self.plane - step * distance, self.plane + step
+
+            def take(origin=origin, ahead=ahead):
+                self.arrived(unit, self.pair, origin, self.core)
+                block = (self.pair, origin, self.core)
+                target = (self.pair, ahead, self.core)
+                pl.when(self.inside(ahead))(
+                    lambda: self.copy(unit, block, self.slot(0, origin), target).start()
+                )
+                self.spread(unit, origin)
+
+            pl.when(self.inside(origin))(take)
+
+    def from_near(self, unit):
+        near, far, _ = self.partners(unit)
+        for plane in range(self.planes):
+            self.arrived(unit, near, plane, self.core)
+            block = (near, plane, self.core)
+            for kind, pair, core in ((3, far, self.core), (5, self.pair, 1 - self.core)):
+                self.copy(unit, block, self.slot(kind, plane), (pair, self.plane, core)).start()
+
+    def from_far(self, unit):
+        _, far, both = self.partners(unit)
+        for kind, pair in ((6, far), (7, both)):
+            for plane in range(self.planes):
+                self.arrived(unit, pair, plane, self.core)
+                block = (pair, plane, self.core)
+                target = (self.pair, self.plane, 1 - self.core)
+                self.copy(unit, block, self.slot(kind, plane), target).start()
+
+    def from_core(self, unit):
+        near, far, both = self.partners(unit)
+        for pair in (self.pair, near, far, both):
+            for plane in range(self.planes):
+                self.arrived(unit, pair, plane, 1 - self.core)
+
+    def drain(self, unit):
+        here = (self.pair, self.plane, self.core)
+
+        def sent(slot):
+            self.copy(unit, here, slot, here, True).wait_send()
+
+        for up in (0, 1):
+            step = 2 * up - 1
+            ahead = self.inside(self.plane + step)
+            pl.when(ahead)(lambda up=up: sent(up))
+            for distance in range(1, self.planes):
+                origin = self.plane - step * distance
+                pl.when(ahead & self.inside(origin))(
+                    lambda origin=origin: sent(self.slot(0, origin))
+                )
+        for kind in range(1, 8):
+            for plane in range(self.planes):
+                sent(self.slot(kind, plane))
+
+
+class Scatter(Route):
+    @staticmethod
+    def slots(planes):
+        return 6 * planes + 3
+
+    @staticmethod
+    def buffers(planes, block, dtype):
+        return [
+            pltpu.VMEM((4, planes, *block), dtype),
+            pltpu.VMEM((2, planes, *block), dtype),
+            pltpu.VMEM((planes, *block), dtype),
+            pltpu.VMEM((2, planes, *block), dtype),
+        ]
+
+    def copy(self, unit, slot, source, target, device):
+        return self.remote(source, target, unit, slot, slot, device)
+
+    def core_copy(self, unit, pair, plane):
+        source = self.units[unit]["place"](pair, plane, 1 - self.core)
+        target = self.units[unit]["core"].at[pair, plane]
+        other = (self.pair, self.plane, 1 - self.core)
+        return self.copy(unit, pair * self.planes + plane, source, target, other)
+
+    def far_copy(self, unit, which, pair):
+        held = self.units[unit]
+        _, far, _ = self.partners(unit)
+        target = (far, self.plane, self.core)
+        slot = 4 * self.planes + which
+        return self.copy(unit, slot, held["core"].at[pair], held["far"].at[which], target)
+
+    def near_copy(self, unit):
+        held = self.units[unit]
+        near, _, _ = self.partners(unit)
+        target = (near, self.plane, self.core)
+        return self.copy(unit, 4 * self.planes + 2, held["far"].at[1], held["near"], target)
+
+    def z_copy(self, unit, up, plane, first):
+        held = self.units[unit]
+        source = held["near"].at[plane] if first else held["z"].at[up, plane]
+        target = (self.pair, self.plane + 2 * up - 1, self.core)
+        slot = 4 * self.planes + 3 + up * self.planes + plane
+        return self.copy(unit, slot, source, held["z"].at[up, plane], target)
+
+    def launch(self, unit, first, count):
+        for i in range(count):
+            place = first + i
+            self.core_copy(unit, place // self.planes, lax.rem(place, self.planes)).start()
+
+    def add(self, target, term_of):
+        def body(i):
+            total = target[i].astype(F32) + term_of(i).astype(F32)
+            target[i] = total.astype(target.dtype)
+
+        loop(self.planes, body)
+
+    def from_core(self, unit):
+        held = self.units[unit]
+        near, far, both = self.partners(unit)
+        for which, pair in ((1, both), (0, far), (None, near), (None, self.pair)):
+            for plane in range(self.planes):
+                self.core_copy(unit, pair, plane).wait_recv()
+            self.add(
+                held["core"].at[pair], lambda i, pair=pair: held["place"](pair, i, self.core)[...]
+            )
+            if which is not None:
+                self.far_copy(unit, which, pair).start()
+
+    def from_far(self, unit):
+        held = self.units[unit]
+        near, far, both = self.partners(unit)
+        self.far_copy(unit, 1, both).wait_recv()
+        self.add(held["far"].at[1], lambda i: held["core"][near, i])
+        self.near_copy(unit).start()
+        self.far_copy(unit, 0, far).wait_recv()
+        self.add(held["far"].at[0], lambda i: held["core"][self.pair, i])
+
+    def z_cases(self, up):
+        step = 2 * up - 1
+        starts = jnp.logical_not(self.inside(self.plane - step))
+        for distance in range(self.planes - 1, 0, -1):
+            target = self.plane + step * distance
+            inside = self.inside(target)
+            yield target, inside & starts, inside & jnp.logical_not(starts)
+
+    def from_near(self, unit):
+        held = self.units[unit]
+        self.near_copy(unit).wait_recv()
+        self.add(held["near"], lambda i: held["far"][0, i])
+        for up in (0, 1):
+            for target, starts, _ in self.z_cases(up):
+                pl.when(starts)(
+                    lambda up=up, target=target: self.z_copy(unit, up, target, True).start()
+                )
+
+    def from_z(self, unit):
+        held = self.units[unit]
+        for cases in zip(self.z_cases(0), self.z_cases(1)):
+            for up, (target, _, passes) in enumerate(cases):
+
+                def go(up=up, target=target):
+                    self.z_copy(unit, up, target, False).wait_recv()
+                    place = held["z"].at[up, target]
+                    total = place[...].astype(F32) + held["near"][target].astype(F32)
+                    place[...] = total.astype(place.dtype)
+                    self.z_copy(unit, up, target, False).start()
+
+                pl.when(passes)(go)
+
+    def finish(self, unit):
+        held = self.units[unit]
+        result = held["result"]
+        result[...] = held["near"][self.plane].astype(F32)
+        for up in (0, 1):
+
+            def take(up=up):
+                self.z_copy(unit, up, self.plane, False).wait_recv()
+                result[...] += held["z"][up, self.plane].astype(F32)
+
+            pl.when(self.inside(self.plane - 2 * up + 1))(take)
+
+    def drain(self, unit):
+        near, far, both = self.partners(unit)
+        for pair in range(4):
+            for plane in range(self.planes):
+                self.core_copy(unit, pair, plane).wait_send()
+        self.far_copy(unit, 1, both).wait_send()
+        self.far_copy(unit, 0, far).wait_send()
+        self.near_copy(unit).wait_send()
+        for up in (0, 1):
+            for target, starts, passes in self.z_cases(up):
+                pl.when(starts | passes)(
+                    lambda up=up, target=target: self.z_copy(unit, up, target, False).wait_send()
+                )
+
+
+def norm_rows(widths):
+    return [-(-width // 128) for width in widths]
+
+
+def unpack_gathered(small, planes, part, lane_rows, lweights, wide, tnorm, lnorm, norm_sum):
+    owners = 4 * planes * 2
+    norm_sum[...] = jnp.zeros_like(norm_sum)
+
+    def body(owner):
+        block = small[owner // (2 * planes), lax.rem(owner // 2, planes), lax.rem(owner, 2)]
+        block = block.astype(F32)
+        for i in range(3):
+            rows = pl.ds(pl.multiple_of(owner * part, part), part)
+            wide[i, rows, :] = block[i * part : (i + 1) * part]
+        norm_sum[...] += block[3 * part : 3 * part + norm_sum.shape[0]]
+
+    loop(owners, body)
+    for i, weight in enumerate(lweights):
+        weight[...] = wide[i].astype(BF16)
+    row = 0
+    for norm, rows in zip((tnorm, lnorm), lane_rows):
+        for i in range(4):
+            for j in range(rows):
+                lanes = min(128, norm.shape[1] - 128 * j)
+                norm[i : i + 1, 128 * j : 128 * j + lanes] = norm_sum[row : row + 1, :lanes]
+                row += 1
+
+
+def pack_grads(small, planes, part, lane_rows, wide, gtnorm, glnorm, norm_sum):
+    norm_sum[...] = jnp.zeros_like(norm_sum)
+    row = 0
+    for norm, rows in zip((gtnorm, glnorm), lane_rows):
+        for i in range(4):
+            for j in range(rows):
+                lanes = min(128, norm.shape[1] - 128 * j)
+                norm_sum[row : row + 1, :lanes] = norm[i : i + 1, 128 * j : 128 * j + lanes]
+                row += 1
+    tail = small.shape[-2] - 3 * part - norm_sum.shape[0]
+
+    def body(owner):
+        rows = pl.ds(pl.multiple_of(owner * part, part), part)
+        pieces = [wide[i, rows, :] for i in range(3)] + [norm_sum[...]]
+        if tail:
+            pieces.append(jnp.zeros((tail, small.shape[-1]), F32))
+        block = jnp.concatenate(pieces, axis=0).astype(BF16)
+        small[owner // (2 * planes), lax.rem(owner // 2, planes), lax.rem(owner, 2)] = block
+
+    loop(4 * planes * 2, body)
+
+
+def spaced(tasks, first, last):
+    by_index = {}
+    for i, task in enumerate(tasks):
+        place = first + (last - first) * i // max(len(tasks) - 1, 1)
+        by_index.setdefault(place, []).append(task)
+    return by_index
+
+
+def heads_beside(body, by_index):
+    def step(head):
+        for place, tasks in sorted(by_index.items()):
+
+            def run(tasks=tasks):
+                for task in tasks:
+                    task()
+
+            pl.when(head == place)(run)
+        body(head)
+
+    loop(HEADS, step)
+
+
+def whole_kernel(planes, dims, scales, chunks, part, lpart, *refs):
+    (
+        lengths, x, y, gx, gy, own, own_small,
+        text_out, layout_out, dx, dy, gown_attn, gown_up, gown_down, gown_small,
+        attn, up, down, small, lattn, lup, ldown, wide, norm_sum,
+        tnorm, lnorm, gtnorm, glnorm,
+        qkv_t, qkv_l, ctx_tt, ctx_tl, ctx_t, ctx_l, act_t, act_l, slope_t, slope_l,
+        dhid_t, dhid_l, hat_t, hat_l, low_t, low_l, dlow_t, dlow_l, rate_t, rate_l, lse,
+        *held,
+    ) = refs
+    local_sem, gsend, grecv, ssend, srecv = held[-5:]
+    widths = (x.shape[1], y.shape[1])
+    lane_rows = norm_rows(widths)
+    length = lengths[0]
+    half_rows = part // 2
+
+    def text_place(whole, half):
+        def place(pair, plane, core):
+            owner = (pair * planes + plane) * 2 + core
+            first = pl.multiple_of(owner * part + half * half_rows, half_rows)
+            return whole.at[pl.ds(first, half_rows), :]
+
+        return place
+
+    def small_place(whole):
+        return lambda pair, plane, core: whole.at[pair, plane, core]
+
+    gunits, sunits = [], []
+    for i, (whole, result) in enumerate(((attn, gown_attn), (up, gown_up), (down, gown_down))):
+        for half in (0, 1):
+            place = text_place(whole, half)
+            gunits.append({"own": own.at[i, half], "place": place, "order": half})
+            at_held = 4 * len(sunits)
+            sunits.append({"place": place, "order": half, "result": result.at[half]})
+            sunits[-1].update(zip(("core", "far", "near", "z"), held[at_held : at_held + 4]))
+    gunits.append({"own": own_small, "place": small_place(small), "order": 0})
+    sunits.append({"place": small_place(small), "order": 1, "result": gown_small})
+    sunits[-1].update(zip(("core", "far", "near", "z"), held[24:28]))
+    ATTN, UP, DOWN, SMALL = (0, 1), (2, 3), (4, 5), 6
+
+    entry_barrier(planes)
+    gather = Gather(planes, gunits, gsend, grecv)
+    scatter = Scatter(planes, sunits, ssend, srecv)
+    here = (gather.pair, gather.plane, gather.core)
+    keeps = [
+        pltpu.make_async_copy(unit["own"], unit["place"](*here), local_sem.at[i])
+        for i, unit in enumerate(gunits)
+    ]
+    for keep in keeps:
+        keep.start()
+
+    def task(step, *args):
+        return lambda: step(*args)
+
+    def every(step, units, *args):
+        for unit in units:
+            step(unit, *args)
+
+    first = (*ATTN, SMALL)
+    every(gather.launch, first)
+    for distance in range(1, planes):
+        every(gather.along, first, distance)
+    every(gather.launch, UP)
+    every(gather.from_near, first)
+    for distance in range(1, planes):
+        every(gather.along, UP, distance)
+    every(gather.from_far, first)
+    every(gather.from_core, first)
+    for unit in first:
+        keeps[unit].wait()
+
+    unpack_gathered(
+        small, planes, lpart, lane_rows, (lattn, lup, ldown), wide, tnorm, lnorm, norm_sum
+    )
+    project_heads(y, lattn, qkv_l, scales[1], chunks[1])
+    project_heads(x, attn, qkv_t, scales[0], chunks[0])
+    early = [task(every, gather.launch, DOWN), *(task(gather.from_near, unit) for unit in UP)]
+    early += [task(every, gather.along, DOWN, distance) for distance in range(1, planes)]
+    late = spaced(early, 0, 5)
+    late[HEADS - 2] = [task(gather.from_far, UP[0])]
+    late[HEADS - 1] = [task(gather.from_far, UP[1])]
+    heads_beside(
+        lambda h: attend_head(h, length, qkv_t, qkv_l, ctx_tt, ctx_tl, lse, dims, widths), late
+    )
+    every(gather.from_near, DOWN)
+    nothing = lambda i, block: None
+    stream_first(y, ctx_tl, ctx_l, lattn, lnorm, dhid_l, hat_l, rate_l, low_l)
+    stream_up(low_l, lup, act_l, slope_l, chunks[1])
+    stream_down(act_l, ldown, dhid_l, chunks[1])
+    stream_second(gy, lnorm, dhid_l, hat_l, layout_out, dhid_l, dlow_l, glnorm)
+    every(gather.from_far, DOWN)
+    stream_inner_back(
+        low_l, dlow_l, lup, ldown, act_l, slope_l, dhid_l, wide.at[1], wide.at[2], chunks[1], nothing
+    )
+    stream_first_back(
+        lnorm, hat_l, rate_l, dhid_l, dlow_l, ctx_l, lattn, ctx_tl, wide.at[0], glnorm
+    )
+    stream_first(x, ctx_tt, ctx_t, attn, tnorm, dhid_t, hat_t, rate_t, low_t)
+    every(gather.from_core, UP)
+    for unit in UP:
+        keeps[unit].wait()
+    stream_up(low_t, up, act_t, slope_t, chunks[0])
+    every(gather.from_core, DOWN)
+    for unit in DOWN:
+        keeps[unit].wait()
+    stream_down(act_t, down, dhid_t, chunks[0])
+    stream_second(gx, tnorm, dhid_t, hat_t, text_out, dhid_t, dlow_t, gtnorm)
+    every(gather.drain, range(len(gunits)))
+
+    by_chunk = chunks[0] // (2 * part)
+
+    def ready(units):
+        return lambda i, block: every(scatter.launch, units, i * by_chunk, by_chunk)
+
+    stream_inner_back(
+        low_t, dlow_t, up, down, act_t, slope_t, dhid_t, up, down, chunks[0], ready((*UP, *DOWN))
+    )
+    stream_first_back(tnorm, hat_t, rate_t, dhid_t, dlow_t, ctx_t, attn, ctx_tt, attn, gtnorm)
+    every(scatter.launch, ATTN, 3 * planes, planes)
+    every(scatter.from_core, (*UP, *DOWN))
+    heads_beside(
+        lambda h: attend_head_back(
+            h, length, qkv_t, qkv_l, ctx_tt, ctx_tl, lse, qkv_t, qkv_l, dims, widths, scales
+        ),
+        {HEADS - 3: [task(scatter.from_far, UP[0])], HEADS - 2: [task(scatter.from_far, UP[1])]},
+    )
+    project_back(y, lattn, qkv_l, dhid_l, dy, wide.at[0], chunks[1], nothing)
+    pack_grads(small, planes, lpart, lane_rows, wide, gtnorm, glnorm, norm_sum)
+    scatter.launch(SMALL, 0, 4 * planes)
+    project_back(x, attn, qkv_t, dhid_t, dx, attn, chunks[0], ready(ATTN))
+    every(scatter.from_far, DOWN)
+    every(scatter.from_core, first)
+    every(scatter.from_near, UP)
+    every(scatter.from_near, DOWN)
+    every(scatter.from_z, UP)
+    every(scatter.from_z, DOWN)
+    every(scatter.finish, (*UP, *DOWN))
+    every(scatter.from_far, first)
+    every(scatter.from_near, first)
+    every(scatter.from_z, first)
+    every(scatter.finish, first)
+    every(scatter.drain, range(len(sunits)))
+
+
+def whole_layer(planes, x, y, lengths, gx, gy, own, own_small, lpart, linner):
+    rows, width = x.shape
+    lwidth = y.shape[1]
+    owners = 4 * planes * 2
+    part = 2 * own.shape[2]
+    inner = owners * part
+    dims = (width // HEADS, lwidth // HEADS)
+    scales = tuple(float(dim) ** -0.5 for dim in dims)
+    vmem = pl.BlockSpec(memory_space=pltpu.VMEM)
+    anywhere = pl.BlockSpec(memory_space=pl.ANY)
+    smem = pl.BlockSpec(memory_space=pltpu.SMEM)
+    like = jax.ShapeDtypeStruct
+    norm_count = 4 * sum(norm_rows((width, lwidth)))
+    small = (4, planes, 2, *own_small.shape)
+
+    def both(shape_of, dtype):
+        return [pltpu.VMEM(shape_of(width, inner), dtype), pltpu.VMEM(shape_of(lwidth, linner), dtype)]
+
+    held = []
+    for _ in range(6):
+        held += Scatter.buffers(planes, own.shape[2:], BF16)
+    held += Scatter.buffers(planes, own_small.shape, BF16)
+    scratch = [
+        pltpu.VMEM((inner, width), BF16),
+        pltpu.VMEM((inner, width), BF16),
+        pltpu.VMEM((inner, width), BF16),
+        pltpu.VMEM(small, BF16),
+        pltpu.VMEM((linner, lwidth), BF16),
+        pltpu.VMEM((linner, lwidth), BF16),
+        pltpu.VMEM((linner, lwidth), BF16),
+        pltpu.VMEM((3, linner, lwidth), F32),
+        pltpu.VMEM((norm_count, lwidth), F32),
+        *both(lambda w, f: (4, w), F32),
+        *both(lambda w, f: (4, w), F32),
+        *both(lambda w, f: (3 * w, rows), BF16),
+        *both(lambda w, f: (w, rows), BF16),
+        *both(lambda w, f: (rows, w), BF16),
+        *both(lambda w, f: (f, rows), BF16),
+        *both(lambda w, f: (f, rows), BF16),
+        *both(lambda w, f: (rows, w), F32),
+        *both(lambda w, f: (rows, w), F32),
+        *both(lambda w, f: (rows, w), BF16),
+        *both(lambda w, f: (rows, w), BF16),
+        *both(lambda w, f: (rows, 1), F32),
+        pltpu.VMEM((HEADS, 1, rows), F32),
+        *held,
+        pltpu.SemaphoreType.DMA((7,)),
+        pltpu.SemaphoreType.DMA((7, Gather.slots(planes))),
+        pltpu.SemaphoreType.DMA((7, owners)),
+        pltpu.SemaphoreType.DMA((7, Scatter.slots(planes))),
+        pltpu.SemaphoreType.DMA((7, Scatter.slots(planes))),
+    ]
+    return pl.pallas_call(
+        functools.partial(whole_kernel, planes, dims, scales, (384, 192), part, lpart),
+        out_shape=[
+            like(x.shape, BF16),
+            like(y.shape, BF16),
+            like(x.shape, BF16),
+            like(y.shape, BF16),
+            *[like(own.shape[1:], F32)] * 3,
+            like(own_small.shape, F32),
+        ],
+        in_specs=[smem] + [vmem] * 4 + [anywhere] * 2,
+        out_specs=[vmem] * 8,
+        scratch_shapes=scratch,
+        compiler_params=pltpu.CompilerParams(
+            collective_id=0, has_side_effects=True, vmem_limit_bytes=67043328
+        ),
+        name="whole_layer",
+    )(lengths, x, y, gx, gy, own, own_small)
+
+
+def pack_small(pieces, norm_part, multiple):
+    owners, _, width = pieces[0].shape
+    norm_part = jnp.pad(norm_part, ((0, 0), (0, -norm_part.shape[1] % width)))
+    block = jnp.concatenate([*pieces, norm_part.reshape(owners, -1, width)], axis=1)
+    return jnp.pad(block, ((0, 0), (0, -block.shape[1] % multiple), (0, 0)))
+
+
+def unpack_small(block, part, count):
+    pieces = [block[:, i * part : (i + 1) * part] for i in range(3)]
+    return pieces, block[:, 3 * part :].reshape(block.shape[0], -1)[:, :count]
+
+
+def lanes_of(flat, widths):
+    pieces, first = [], 0
+    for width in widths:
+        piece = flat[first : first + 4 * width].reshape(4, width)
+        first += 4 * width
+        pieces.append(jnp.pad(piece, ((0, 0), (0, -width % 128))).reshape(-1, 128))
+    return jnp.concatenate(pieces, axis=0)
+
+
+def flat_of(lanes, widths):
+    pieces, first = [], 0
+    for width, rows in zip(widths, norm_rows(widths)):
+        piece = lanes[first : first + 4 * rows].reshape(4, rows * 128)
+        first += 4 * rows
+        pieces.append(piece[:, :width].reshape(-1))
+    return jnp.concatenate(pieces)
+
+
+def by_kernel(
+    planes, text_in, layout_in, lengths, attn_text, up_text, down_text,
+    attn_layout, up_layout, down_layout, norm_params, grad_text, grad_layout,
+):
+    width, lwidth = text_in.shape[1], layout_in.shape[1]
+    owners = lax.axis_size(AXES)
+    text_part, part = down_text.shape[0], down_layout.shape[0]
+    count = norm_params.shape[0]
+    own = jnp.stack([attn_text.T, up_text.T, down_text]).reshape(3, 2, text_part // 2, width)
+    first = lax.axis_index(AXES) * count
+    spread = jnp.pad(norm_params, ((owners - 1) * count, (owners - 1) * count))
+    spread = lax.dynamic_slice(spread, ((owners - 1) * count - first,), (owners * count,))
+    lanes = lanes_of(spread, (width, lwidth))
+    lanes = jnp.pad(lanes, ((0, 0), (0, lwidth - 128)))
+    small = jnp.concatenate([attn_layout.T, up_layout.T, down_layout, lanes], axis=0)
+    small = jnp.pad(small, ((0, -small.shape[0] % 16), (0, 0)))
+    text_out, layout_out, dx, dy, gattn, gup, gdown, gsmall = whole_layer(
+        planes, text_in, layout_in, lengths, grad_text, grad_layout, own, small,
+        part, owners * part,
+    )
+    gattn, gup, gdown = (grad.reshape(text_part, width) for grad in (gattn, gup, gdown))
+    glattn, glup, gldown = (gsmall[i * part : (i + 1) * part] for i in range(3))
+    gnorm = gsmall[3 * part : 3 * part + lanes.shape[0], :128]
+    gnorm = lax.dynamic_slice(flat_of(gnorm, (width, lwidth)), (first,), (count,))
+    return text_out, layout_out, dx, dy, gattn.T, gup.T, gdown, glattn.T, glup.T, gldown, gnorm
+
+
+def by_collectives(
     text_in, layout_in, lengths, attn_text, up_text, down_text,
     attn_layout, up_layout, down_layout, norm_params, grad_text, grad_layout,
 ):
     width, lwidth = text_in.shape[1], layout_in.shape[1]
     owners = lax.axis_size(AXES)
-    part = down_layout.shape[0]
-    count = norm_params.shape[0]
+    part, count = down_layout.shape[0], norm_params.shape[0]
 
     def gather(piece):
         return lax.all_gather(piece, AXES, axis=0, tiled=True)
 
-    attn, up, down = gather(attn_text.T), gather(up_text.T), gather(down_text)
-    norm_row = jnp.pad(norm_params, (0, -count % lwidth)).reshape(-1, lwidth)
-    small = gather(jnp.concatenate([attn_layout.T, up_layout.T, down_layout, norm_row], axis=0))
-    nrows = norm_row.shape[0]
-    small = small.reshape(owners, 3 * part + nrows, lwidth)
-    lattn, lup, ldown = (
-        small[:, i * part : (i + 1) * part].reshape(owners * part, lwidth) for i in range(3)
-    )
-    norms = small[:, 3 * part :].reshape(owners, -1)[:, :count].reshape(-1).astype(F32)
+    def scatter(piece):
+        return lax.psum_scatter(piece, AXES, scatter_dimension=0, tiled=True)
+
+    small = pack_small(
+        [attn_layout.T[None], up_layout.T[None], down_layout[None]], norm_params[None], 16
+    )
+    pieces, norms = unpack_small(gather(small), part, count)
+    lattn, lup, ldown = (piece.reshape(owners * part, lwidth) for piece in pieces)
+    norms = norms.reshape(-1).astype(F32)
     tnorm = norms[: 4 * width].reshape(4, width)
     lnorm = norms[4 * width :].reshape(4, lwidth)
+    attn, up, down = gather(attn_text.T), gather(up_text.T), gather(down_text)
     (
         text_out, layout_out, dx, dy, gattn, gup, gdown, glattn, glup, gldown, gtnorm, glnorm,
     ) = layer(
         text_in, layout_in, lengths, grad_text, grad_layout, tnorm, lnorm,
         attn, up, down, lattn, lup, ldown,
     )
-
-    def scatter(piece):
-        return lax.psum_scatter(piece, AXES, scatter_dimension=0, tiled=True)
-
     gnorm = jnp.concatenate([gtnorm.reshape(-1), glnorm.reshape(-1)]).reshape(owners, count)
-    gsmall = jnp.concatenate(
-        [piece.reshape(owners, part, lwidth) for piece in (glattn, glup, gldown)]
-        + [jnp.pad(gnorm, ((0, 0), (0, -count % lwidth))).reshape(owners, nrows, lwidth)],
-        axis=1,
-    )
-    gsmall = scatter(gsmall.reshape(-1, lwidth))
-    gattn, gup, gdown = (scatter(piece).astype(F32) for piece in (gattn, gup, gdown))
+    gsmall = pack_small(
+        [piece.reshape(owners, part, lwidth) for piece in (glattn, glup, gldown)], gnorm, 16
+    )
+    gattn, gup, gdown, gsmall = (
+        scatter(grad).astype(F32) for grad in (gattn, gup, gdown, gsmall)
+    )
+    (glattn, glup, gldown), gnorm = unpack_small(gsmall, part, count)
     return (
-        text_out,
-        layout_out,
-        dx,
-        dy,
-        gattn.T,
-        gup.T,
-        gdown,
-        gsmall[:part].T,
-        gsmall[part : 2 * part].T,
-        gsmall[2 * part : 3 * part],
-        gsmall[3 * part :].reshape(-1)[:count],
+        text_out, layout_out, dx, dy, gattn.T, gup.T, gdown,
+        glattn[0].T, glup[0].T, gldown[0], gnorm[0],
     )
 
 
 def solution(mesh):
+    pairs, columns_on_axis = mesh.shape["dp"], mesh.shape["fsdp"]
+    body = by_collectives
+    if pairs == 4 and columns_on_axis % 2 == 0 and columns_on_axis <= 8:
+        body = functools.partial(by_kernel, columns_on_axis // 2)
     rows, columns = P(AXES, None), P(None, AXES)
     split = P(AXES)
     return jax.shard_map(
-        per_device,
+        body,
         mesh=mesh,
         in_specs=(
             rows, rows, split, columns, columns, rows, columns, columns, rows, split, rows, rows,

time: 776 us -> 230 us (0.30)
  waiting for transfers between devices: 605 us -> 0 us
  Pallas kernels: 82.1 us -> 210 us
  blocking collectives: 52.9 us -> 0 us
  between operations: 14.9 us -> 1.38 us
    reduce_scatter x3 -> x0, waiting for transfers between devices: 331 us -> none  [scatter(): return lax.psum_scatter(piece, AXES, scatter_dimension=0, tiled=True)]
    all_gather x3 -> x0, waiting for transfers between devices: 140 us -> none  [gather(): return lax.all_gather(piece, AXES, axis=0, tiled=True)]
    unnamed x8 -> x0, waiting for transfers between devices: 134 us -> none
    pallas_call x1, Pallas kernels: 82.1 us -> 210 us  [whole_layer(): pl.pallas_call(functools.partial(whole_kernel, planes, dims, scales, (384...]
    all_gather x1 -> x0, blocking collectives: 52.9 us -> none  [gather(): return lax.all_gather(piece, AXES, axis=0, tiled=True)]
  transfers between devices with their start and end apart: 7 -> 0, of which waited for: 7 -> 0; matrix products, arithmetic and copies ran while one was open for 2% -> 0% of each run, Pallas kernels for 0% -> 0%
where the time goes in v3:
time: 230 us
  Pallas kernels  210 us (91%)
  local copies, waits for them, and re-layouts  15.5 us (7%)
  other arithmetic  2.78 us (1%)
    pallas_call x1, Pallas kernels, whole_layer(): pl.pallas_call(functools.partial(whole_kernel, planes, dims, scales, (384...  210 us
    unnamed x29, local copies, waits for them, and re-layouts  11 us

profile of v3, /device:TPU:0, one launch (start us, length us, event | category | flops | bytes accessed | tf_op | source)
XLA Modules:
  0.0 229.8 jit_solution(2754204086098644513)
XLA Ops:
  1.3 0.7 pad_dynamic-slice_fusion.1
  2.1 0.1 reshape.69
  2.2 0.7 fusion.10
  2.9 1.4 fusion.6.refs_6_
  4.3 0.8 copy.23.refs_2_
  5.3 0.8 copy.24.refs_4_
  6.2 0.2 copy-done.9
  6.4 0.8 pad_maximum_fusion.refs_5_
  7.2 210.2 %whole_layer.1 = (bf16[512,768]{1,0:T(8,128)(2,1)}, bf16[512,192]{1,0:T(8,128)(2,1)}, bf16[512,768]{1,0:T(8,128)(2,1)}, bf16[512,192]{1,0:T(8,128)(2,1)}, f32[2,...) custom-call(s32[1]{0:T(128)S(6)} %copy.32.refs_0_, ...), custom_call_target="tpu_custom_call" | custom-call | tf_op jit(solution)/shard_map/whole_layer/pallas_call | solution.py:923
  217.4 0.7 slice.52
  218.2 0.7 slice_bitcast_fusion.2
  218.9 1.4 fusion.12
  220.3 0.6 fusion.11
  220.9 1.8 copy.25
  222.7 1.8 copy.26
  224.4 0.9 copy.33
  225.3 0.5 copy-done
  225.9 0.9 copy.34
  226.7 0.2 copy-done.4
  227.0 0.7 copy.35
  227.7 0.4 copy-done.3
  228.1 0.7 copy.36
  228.8 0.4 copy-done.2
  229.1 0.7 copy.37
  (20 shorter events, 0.4 us)
Async XLA Ops:
  0.6 3.7 %copy-start.5 = (bf16[512,192]{0,1:T(8,128)(2,1)S(1)}, bf16[512,192]{0,1:T(8,128)(2,1)}, u32[]{:S(2)}) copy-start(bf16[512,192]{0,1:T(8,128)(2,1)} %param.13) | copy-start | bytes 589828
  4.3 0.9 copy-start.6
  5.3 0.9 copy-start.7
  5.3 1.0 copy-start.8
  5.3 1.1 copy-start.9
  217.4 7.1 %copy-start.1 = (bf16[512,768]{1,0:T(8,128)(2,1)S(1)}, bf16[512,768]{1,0:T(8,128)(2,1)}, u32[]{:S(2)}) copy-start(bf16[512,768]{1,0:T(8,128)(2,1)} %get-tuple-element.52) | copy-start | bytes 2359300
  224.4 1.4 copy-start
  225.9 1.1 copy-start.4
  227.0 1.1 copy-start.3
  228.1 1.1 copy-start.2

commit v4 on v3

--- a/solution.py
+++ b/solution.py
@@ -176,8 +176,8 @@
         block = at(i, ROW_STEP)
         hidden = hat[block, :] * norms[0:1, :] + norms[1:2, :] + acc[block, :]
         hat_b, rate_b = normed(hidden)
+        grad = g[block, :].astype(F32)
         out[block, :] = (hat_b * norms[2:3, :] + norms[3:4, :]).astype(BF16)
-        grad = g[block, :].astype(F32)
         back = norm_back(grad, hat_b, rate_b, norms[2:3, :])
         dhid[block, :] = back
         dlow[block, :] = back.astype(BF16)
@@ -189,11 +189,13 @@
     gnorm[3:4, :] = sums[1]
 
 
-def stream_inner_back(low, dlow, up, down, act, slope, dhid, gup, gdown, chunk, done):
+def stream_inner_back(
+    low, dlow, up, down, act, slope, dhid, gup, gdown, chunk, done, chunk_of=lambda i: i
+):
     count, size = steps(up.shape[0], chunk)
 
     def body(i):
-        block = at(i, size)
+        block = at(chunk_of(i), size)
         dact = mm(down[block, :], dlow[...], 1, 1)
         dinner = (dact * slope[block, :].astype(F32)).astype(BF16)
         dhid[...] += mm(dinner, up[block, :], 0, 0)
@@ -369,6 +371,116 @@
     )(lengths, x, y, gx, gy, tnorm, lnorm, attn, up, down, lattn, lup, ldown)
 
 
+SECOND_APART = True
+
+GATHER_PLAN = (
+    (0, "launch", 7),
+    (0, "launch", 3),
+    (0, "along", 3, 1),
+    (0, "launch", 5),
+    (0, "launch", 2),
+    (1, "from_near", 7),
+    (1, "along", 2, 1),
+    (2, "launch", 4),
+    (3, "along", 2, 2),
+    (4, "along", 3, 2),
+    (4, "from_far", 7),
+    (5, "along", 4, 1),
+    (7, "along", 7, 1),
+    (8, "along", 2, 3),
+    (8, "along", 3, 3),
+    (10, "from_near", 2),
+    (10, "from_near", 3),
+    (11, "along", 7, 2),
+    (13, "along", 5, 1),
+    (13, "along", 7, 3),
+    (13, "along", 5, 2),
+    (14, "along", 4, 2),
+    (15, "from_far", 2),
+    (16, "from_far", 3),
+    (16, "along", 5, 3),
+    (16, "along", 4, 3),
+    (19, "from_near", 4),
+    (19, "from_near", 5),
+    (20, "from_far", 5),
+    (20, "from_far", 4),
+)
+SCATTER_PLAN = (
+    (2, "from_core", 2, 0),
+    (3, "from_core", 3, 0),
+    (4, "from_core", 4, 0),
+    (5, "from_core", 2, 1),
+    (5, "from_core", 5, 0),
+    (7, "from_core", 4, 1),
+    (7, "from_core", 3, 1),
+    (9, "from_core", 3, 2),
+    (9, "from_core", 4, 2),
+    (11, "from_core", 5, 1),
+    (11, "from_core", 3, 3),
+    (11, "from_core", 7, 0),
+    (11, "from_core", 7, 1),
+    (11, "from_core", 7, 2),
+    (12, "from_core", 7, 3),
+    (13, "from_core", 5, 2),
+    (13, "from_core", 2, 2),
+    (14, "from_far", 3),
+    (15, "from_core", 5, 3),
+    (15, "from_core", 4, 3),
+    (17, "from_core", 2, 3),
+    (19, "from_far", 4),
+    (20, "from_z", 7, 1),
+    (21, "from_near", 3),
+    (23, "from_far", 2),
+    (25, "from_core", 6, 0),
+    (25, "from_core", 6, 1),
+    (25, "from_core", 6, 2),
+    (25, "from_core", 6, 3),
+    (25, "from_z", 7, 2),
+    (27, "from_near", 4),
+    (27, "from_far", 5),
+    (29, "from_near", 2),
+    (30, "from_z", 3, 1),
+    (30, "from_far", 6),
+    (30, "finish", 7),
+    (31, "from_z", 3, 2),
+    (31, "from_near", 5),
+    (31, "from_z", 4, 1),
+    (31, "from_far", 7),
+    (31, "from_near", 6),
+    (31, "from_z", 2, 1),
+    (32, "from_core", 0, 0),
+    (32, "from_core", 1, 0),
+    (32, "from_near", 7),
+    (32, "from_z", 6, 1),
+    (32, "from_core", 0, 1),
+    (32, "from_z", 5, 1),
+    (32, "from_core", 0, 2),
+    (32, "from_z", 6, 2),
+    (32, "from_z", 2, 2),
+    (32, "from_core", 0, 3),
+    (32, "from_core", 1, 1),
+    (32, "from_far", 0),
+    (32, "from_core", 1, 2),
+    (32, "from_z", 4, 2),
+    (32, "from_core", 1, 3),
+    (32, "from_z", 5, 2),
+    (32, "from_near", 0),
+    (32, "from_z", 0, 1),
+    (32, "finish", 4),
+    (32, "finish", 6),
+    (32, "from_far", 1),
+    (32, "from_z", 0, 2),
+    (32, "from_near", 1),
+    (32, "from_z", 1, 1),
+    (32, "finish", 3),
+    (32, "finish", 2),
+    (32, "finish", 5),
+    (32, "from_z", 1, 2),
+    (32, "finish", 0),
+    (32, "finish", 1),
+)
+
+
 def coordinates(planes):
     pair, column = lax.axis_index("dp"), lax.axis_index("fsdp")
     x, y = lax.rem(pair, 2), pair // 2
@@ -408,6 +520,14 @@
         order = self.units[unit]["order"]
         near, far = self.across[order], self.across[1 - order]
         return near, far, self.across[0] + self.across[1] - self.pair
+
+    def turn(self, index):
+        near, far = self.across
+        order = (near + far - self.pair, far, near, self.pair)
+        if isinstance(index, int):
+            return order[index]
+        later = jnp.where(index == 2, order[2], order[3])
+        return jnp.where(index == 0, order[0], jnp.where(index == 1, order[1], later))
 
     def inside(self, plane):
         return (plane >= 0) & (plane < self.planes)
@@ -424,84 +544,131 @@
 
 
 class Gather(Route):
-    def copy(self, unit, block, slot, target, own=False):
-        pair, plane, core = block
+    @staticmethod
+    def send_slots(planes):
+        return 3 + planes
+
+    @staticmethod
+    def arrival_slots(planes):
+        return 5 * planes + 1
+
+    def copy(self, unit, block, slot, arrival, target, own=False):
         place = self.units[unit]["place"](*block)
         source = self.units[unit]["own"] if own else place
-        arrival = (pair * self.planes + plane) * 2 + core
         return self.remote(source, place, unit, slot, arrival, target)
 
-    def arrived(self, unit, pair, plane, core):
+    def arrival(self, block):
+        return block[0] * self.planes + block[1]
+
+    def share(self, unit, block, pair, own=False):
+        target = (pair, self.plane, self.core)
+        self.copy(unit, block, 2 + self.planes, self.arrival(block), target, own).start()
+
+    def to_core(self, unit, block, own=False):
+        target = (self.pair, self.plane, 1 - self.core)
+        self.copy(unit, block, 2 + self.planes, 5 * self.planes, target, own).start()
+
+    def arrived(self, unit, pair, plane):
         here = (self.pair, self.plane, self.core)
-        self.copy(unit, (pair, plane, core), 0, here).wait_recv()
-
-    def slot(self, kind, plane):
-        return 2 + kind * self.planes + plane
-
-    @staticmethod
-    def slots(planes):
-        return 2 + 8 * planes
+        block = (pair, plane, self.core)
+        self.copy(unit, block, 0, self.arrival(block), here).wait_recv()
+
+    def wait_blocks(self, unit, count, semaphore):
+        sized = self.units[unit]["sized"](count)
+        pltpu.make_async_copy(sized, sized, semaphore).wait()
+
+    def ahead(self, step):
+        return (self.pair, self.plane + step, self.core)
 
     def spread(self, unit, plane, own=False):
         near, far, _ = self.partners(unit)
         block = (self.pair, plane, self.core)
-        for kind, pair, core in ((1, near, self.core), (2, far, self.core), (4, self.pair, 1 - self.core)):
-            self.copy(unit, block, self.slot(kind, plane), (pair, self.plane, core), own).start()
+        self.share(unit, block, near, own)
+        self.share(unit, block, far, own)
+        self.to_core(unit, block, own)
 
     def launch(self, unit):
         block = (self.pair, self.plane, self.core)
-        for up in (0, 1):
-            ahead = self.plane + 2 * up - 1
-            pl.when(self.inside(ahead))(
-                lambda up=up, ahead=ahead: self.copy(
-                    unit, block, up, (self.pair, ahead, self.core), True
+        if not self.units[unit]["z_last"]:
+            for up in (0, 1):
+                step = 2 * up - 1
+                send = lambda up=up, step=step: self.copy(
+                    unit, block, up, self.arrival(block), self.ahead(step), True
                 ).start()
-            )
+                pl.when(self.inside(self.plane + step))(send)
         self.spread(unit, self.plane, True)
 
+    def four(self, unit, plane, slot, step):
+        for pair in range(4):
+            block = (pair, plane, self.core)
+            self.copy(unit, block, slot, 4 * self.planes + plane, self.ahead(step)).start()
+
     def along(self, unit, distance):
+        z_last = self.units[unit]["z_last"]
         for step in (-1, 1):
-            origin, ahead = self.plane - step * distance, self.plane + step
-
-            def take(origin=origin, ahead=ahead):
-                self.arrived(unit, self.pair, origin, self.core)
+            origin = self.plane - step * distance
+            onward = self.inside(self.plane + step)
+
+            def take(origin=origin, step=step, onward=onward):
+                if z_last:
+                    self.wait_blocks(unit, 4, self.recv_sem.at[unit, 4 * self.planes + origin])
+                    pl.when(onward)(lambda: self.four(unit, origin, 2 + origin, step))
+                    for pair in range(4):
+                        self.to_core(unit, (pair, origin, self.core))
+                    return
+                self.arrived(unit, self.pair, origin)
                 block = (self.pair, origin, self.core)
-                target = (self.pair, ahead, self.core)
-                pl.when(self.inside(ahead))(
-                    lambda: self.copy(unit, block, self.slot(0, origin), target).start()
-                )
+                send = lambda: self.copy(
+                    unit, block, 2 + origin, self.arrival(block), self.ahead(step)
+                ).start()
+                pl.when(onward)(send)
                 self.spread(unit, origin)
 
             pl.when(self.inside(origin))(take)
+
+    def planes_here(self, unit):
+        return (self.plane,) if self.units[unit]["z_last"] else range(self.planes)
 
     def from_near(self, unit):
         near, far, _ = self.partners(unit)
-        for plane in range(self.planes):
-            self.arrived(unit, near, plane, self.core)
-            block = (near, plane, self.core)
-            for kind, pair, core in ((3, far, self.core), (5, self.pair, 1 - self.core)):
-                self.copy(unit, block, self.slot(kind, plane), (pair, self.plane, core)).start()
+        for plane in self.planes_here(unit):
+            self.arrived(unit, near, plane)
+            self.share(unit, (near, plane, self.core), far)
+            self.to_core(unit, (near, plane, self.core))
 
     def from_far(self, unit):
         _, far, both = self.partners(unit)
-        for kind, pair in ((6, far), (7, both)):
-            for plane in range(self.planes):
-                self.arrived(unit, pair, plane, self.core)
-                block = (pair, plane, self.core)
-                target = (self.pair, self.plane, 1 - self.core)
-                self.copy(unit, block, self.slot(kind, plane), target).start()
+        for pair in (far, both):
+            for plane in self.planes_here(unit):
+                self.arrived(unit, pair, plane)
+                self.to_core(unit, (pair, plane, self.core))
+        if self.units[unit]["z_last"]:
+            self.keep_own(unit)
+            for up in (0, 1):
+                step = 2 * up - 1
+                pl.when(self.inside(self.plane + step))(
+                    lambda up=up, step=step: self.four(unit, self.plane, up, step)
+                )
+
+    def keep(self, unit):
+        here = (self.pair, self.plane, self.core)
+        source, place = self.units[unit]["own"], self.units[unit]["place"](*here)
+        return pltpu.make_async_copy(source, place, self.units[unit]["keep_sem"])
+
+    def keep_own(self, unit):
+        self.keep(unit).wait()
 
     def from_core(self, unit):
-        near, far, both = self.partners(unit)
-        for pair in (self.pair, near, far, both):
-            for plane in range(self.planes):
-                self.arrived(unit, pair, plane, 1 - self.core)
+        if not self.units[unit]["z_last"]:
+            self.keep_own(unit)
+        self.wait_blocks(unit, 4 * self.planes, self.recv_sem.at[unit, 5 * self.planes])
 
     def drain(self, unit):
-        here = (self.pair, self.plane, self.core)
+        z_last = self.units[unit]["z_last"]
+        along = 4 if z_last else 1
 
         def sent(slot):
-            self.copy(unit, here, slot, here, True).wait_send()
+            self.wait_blocks(unit, along, self.send_sem.at[unit, slot])
 
         for up in (0, 1):
             step = 2 * up - 1
@@ -509,89 +676,100 @@
             pl.when(ahead)(lambda up=up: sent(up))
             for distance in range(1, self.planes):
                 origin = self.plane - step * distance
-                pl.when(ahead & self.inside(origin))(
-                    lambda origin=origin: sent(self.slot(0, origin))
-                )
-        for kind in range(1, 8):
-            for plane in range(self.planes):
-                sent(self.slot(kind, plane))
+                pl.when(ahead & self.inside(origin))(lambda origin=origin: sent(2 + origin))
+        shared = 3 + 4 * self.planes if z_last else 7 * self.planes
+        self.wait_blocks(unit, shared, self.send_sem.at[unit, 2 + self.planes])
 
 
 class Scatter(Route):
     @staticmethod
-    def slots(planes):
-        return 6 * planes + 3
+    def send_slots(planes):
+        return 3 + 3 * planes
 
     @staticmethod
-    def buffers(planes, block, dtype):
-        return [
-            pltpu.VMEM((4, planes, *block), dtype),
-            pltpu.VMEM((2, planes, *block), dtype),
-            pltpu.VMEM((planes, *block), dtype),
-            pltpu.VMEM((2, planes, *block), dtype),
-        ]
-
-    def copy(self, unit, slot, source, target, device):
-        return self.remote(source, target, unit, slot, slot, device)
+    def arrival_slots(planes):
+        return 6 + 3 * planes
+
+    @staticmethod
+    def buffers(planes, block, z_first):
+        shapes = [(4, planes), (2, planes), (planes,), (2, planes)]
+        if z_first:
+            shapes = [(4, planes), (2, 1), (1,), (2, planes, 4)]
+        return [pltpu.VMEM((*shape, *block), BF16) for shape in shapes]
 
     def core_copy(self, unit, pair, plane):
         source = self.units[unit]["place"](pair, plane, 1 - self.core)
         target = self.units[unit]["core"].at[pair, plane]
         other = (self.pair, self.plane, 1 - self.core)
-        return self.copy(unit, pair * self.planes + plane, source, target, other)
+        return self.remote(source, target, unit, 0, pair, other)
 
     def far_copy(self, unit, which, pair):
         held = self.units[unit]
         _, far, _ = self.partners(unit)
         target = (far, self.plane, self.core)
-        slot = 4 * self.planes + which
-        return self.copy(unit, slot, held["core"].at[pair], held["far"].at[which], target)
-
-    def near_copy(self, unit):
+        source = held["core"].at[pair]
+        if held["z_first"]:
+            source = source.at[pl.ds(self.plane, 1)]
+        return self.remote(source, held["far"].at[which], unit, 1 + which, 4 + which, target)
+
+    def near_copy(self, unit, plane):
         held = self.units[unit]
         near, _, _ = self.partners(unit)
         target = (near, self.plane, self.core)
-        return self.copy(unit, 4 * self.planes + 2, held["far"].at[1], held["near"], target)
+        source, place = held["far"].at[1, plane], held["near"].at[plane]
+        return self.remote(source, place, unit, 3 + plane, 6 + plane, target)
 
     def z_copy(self, unit, up, plane, first):
         held = self.units[unit]
-        source = held["near"].at[plane] if first else held["z"].at[up, plane]
+        source = held["z"].at[up, plane]
+        if first:
+            source = held["core"].at[:, plane] if held["z_first"] else held["near"].at[plane]
         target = (self.pair, self.plane + 2 * up - 1, self.core)
-        slot = 4 * self.planes + 3 + up * self.planes + plane
-        return self.copy(unit, slot, source, held["z"].at[up, plane], target)
-
-    def launch(self, unit, first, count):
-        for i in range(count):
-            place = first + i
-            self.core_copy(unit, place // self.planes, lax.rem(place, self.planes)).start()
-
-    def add(self, target, term_of):
-        def body(i):
-            total = target[i].astype(F32) + term_of(i).astype(F32)
-            target[i] = total.astype(target.dtype)
-
-        loop(self.planes, body)
-
-    def from_core(self, unit):
+        line = (1 + up) * self.planes + plane
+        return self.remote(source, held["z"].at[up, plane], unit, 3 + line, 6 + line, target)
+
+    def launch(self, unit, pair, planes=None):
+        for plane in range(self.planes) if planes is None else planes:
+            self.core_copy(unit, pair, plane).start()
+
+    def add(self, target, term):
+        target[...] = (target[...].astype(F32) + term[...].astype(F32)).astype(target.dtype)
+
+    def add_each(self, count, target_of, term_of):
+        loop(count, lambda i: self.add(target_of(i), term_of(i)))
+
+    def from_core(self, unit, turn):
         held = self.units[unit]
-        near, far, both = self.partners(unit)
-        for which, pair in ((1, both), (0, far), (None, near), (None, self.pair)):
-            for plane in range(self.planes):
-                self.core_copy(unit, pair, plane).wait_recv()
-            self.add(
-                held["core"].at[pair], lambda i, pair=pair: held["place"](pair, i, self.core)[...]
-            )
-            if which is not None:
-                self.far_copy(unit, which, pair).start()
+        pair = self.turn(turn)
+        arrived = held["core"].at[pair]
+        pltpu.make_async_copy(arrived, arrived, self.recv_sem.at[unit, pair]).wait()
+        self.add_each(
+            self.planes, lambda i: arrived.at[i], lambda i: held["place"](pair, i, self.core)
+        )
+        if held["z_first"]:
+            if turn == 3:
+                self.start_z(unit, range(self.planes))
+        elif turn == 0:
+            self.far_copy(unit, 1, pair).start()
+        elif turn == (1 if held["order"] == 0 else 2):
+            self.far_copy(unit, 0, pair).start()
 
     def from_far(self, unit):
         held = self.units[unit]
         near, far, both = self.partners(unit)
+        mine = (lambda pair, i: held["core"].at[pair, self.plane]) if held["z_first"] else (
+            lambda pair, i: held["core"].at[pair, i]
+        )
+        count = held["near"].shape[0]
         self.far_copy(unit, 1, both).wait_recv()
-        self.add(held["far"].at[1], lambda i: held["core"][near, i])
-        self.near_copy(unit).start()
+        for plane in self.ends_first(count):
+            self.add(held["far"].at[1, plane], mine(near, plane))
+            self.near_copy(unit, plane).start()
         self.far_copy(unit, 0, far).wait_recv()
-        self.add(held["far"].at[0], lambda i: held["core"][self.pair, i])
+        self.add_each(count, lambda i: held["far"].at[0, i], lambda i: mine(self.pair, i))
+
+    def ends_first(self, count):
+        return sorted(range(count), key=lambda plane: min(plane, count - 1 - plane))
 
     def z_cases(self, up):
         step = 2 * up - 1
@@ -601,50 +779,77 @@
             inside = self.inside(target)
             yield target, inside & starts, inside & jnp.logical_not(starts)
 
+    def start_z(self, unit, planes):
+        for target in planes:
+            for up, end, ahead in ((1, 0, target > 0), (0, self.planes - 1, target < self.planes - 1)):
+                if ahead:
+                    pl.when(self.plane == end)(
+                        lambda up=up, target=target: self.z_copy(unit, up, target, True).start()
+                    )
+
     def from_near(self, unit):
         held = self.units[unit]
-        self.near_copy(unit).wait_recv()
-        self.add(held["near"], lambda i: held["far"][0, i])
+        for plane in self.ends_first(held["near"].shape[0]):
+            self.near_copy(unit, plane).wait_recv()
+            self.add(held["near"].at[plane], held["far"].at[0, plane])
+            if not held["z_first"]:
+                self.start_z(unit, (plane,))
+        if held["z_first"]:
+            held["result"][...] = held["near"][0].astype(F32)
+
+    def from_z(self, unit, hop):
         for up in (0, 1):
-            for target, starts, _ in self.z_cases(up):
-                pl.when(starts)(
-                    lambda up=up, target=target: self.z_copy(unit, up, target, True).start()
-                )
-
-    def from_z(self, unit):
+            come = self.plane if up else self.planes - 1 - self.plane
+            step = 2 * up - 1
+
+            def go(up=up, step=step):
+                for distance in range(self.planes - 1 - hop, 0, -1):
+                    self.z_pass(unit, up, self.plane + step * distance)
+
+            pl.when(come == hop)(go)
+
+    def z_pass(self, unit, up, target):
         held = self.units[unit]
-        for cases in zip(self.z_cases(0), self.z_cases(1)):
-            for up, (target, _, passes) in enumerate(cases):
-
-                def go(up=up, target=target):
-                    self.z_copy(unit, up, target, False).wait_recv()
-                    place = held["z"].at[up, target]
-                    total = place[...].astype(F32) + held["near"][target].astype(F32)
-                    place[...] = total.astype(place.dtype)
-                    self.z_copy(unit, up, target, False).start()
-
-                pl.when(passes)(go)
+        self.z_copy(unit, up, target, False).wait_recv()
+        place = held["z"].at[up, target]
+        if held["z_first"]:
+            self.add_each(4, lambda i: place.at[i], lambda i: held["core"].at[i, target])
+        else:
+            self.add(place, held["near"].at[target])
+        self.z_copy(unit, up, target, False).start()
 
     def finish(self, unit):
         held = self.units[unit]
-        result = held["result"]
-        result[...] = held["near"][self.plane].astype(F32)
+        z_first = held["z_first"]
+        if not z_first:
+            held["result"][...] = held["near"][self.plane].astype(F32)
         for up in (0, 1):
 
             def take(up=up):
                 self.z_copy(unit, up, self.plane, False).wait_recv()
-                result[...] += held["z"][up, self.plane].astype(F32)
+                if z_first:
+                    self.add_each(
+                        4,
+                        lambda i: held["core"].at[i, self.plane],
+                        lambda i: held["z"].at[up, self.plane, i],
+                    )
+                else:
+                    held["result"][...] += held["z"][up, self.plane].astype(F32)
 
             pl.when(self.inside(self.plane - 2 * up + 1))(take)
+        if z_first:
+            _, far, both = self.partners(unit)
+            self.far_copy(unit, 1, both).start()
+            self.far_copy(unit, 0, far).start()
 
     def drain(self, unit):
-        near, far, both = self.partners(unit)
-        for pair in range(4):
-            for plane in range(self.planes):
-                self.core_copy(unit, pair, plane).wait_send()
+        _, far, both = self.partners(unit)
+        core = self.units[unit]["core"]
+        pltpu.make_async_copy(core, core, self.send_sem.at[unit, 0]).wait()
         self.far_copy(unit, 1, both).wait_send()
         self.far_copy(unit, 0, far).wait_send()
-        self.near_copy(unit).wait_send()
+        for plane in range(self.units[unit]["near"].shape[0]):
+            self.near_copy(unit, plane).wait_send()
         for up in (0, 1):
             for target, starts, passes in self.z_cases(up):
                 pl.when(starts | passes)(
@@ -656,79 +861,98 @@
     return [-(-width // 128) for width in widths]
 
 
-def unpack_gathered(small, planes, part, lane_rows, lweights, wide, tnorm, lnorm, norm_sum):
-    owners = 4 * planes * 2
-    norm_sum[...] = jnp.zeros_like(norm_sum)
-
+def unpack_first(small, part, weight, wide):
     def body(owner):
-        block = small[owner // (2 * planes), lax.rem(owner // 2, planes), lax.rem(owner, 2)]
-        block = block.astype(F32)
-        for i in range(3):
-            rows = pl.ds(pl.multiple_of(owner * part, part), part)
-            wide[i, rows, :] = block[i * part : (i + 1) * part]
-        norm_sum[...] += block[3 * part : 3 * part + norm_sum.shape[0]]
-
-    loop(owners, body)
-    for i, weight in enumerate(lweights):
-        weight[...] = wide[i].astype(BF16)
+        rows = pl.ds(pl.multiple_of(owner * part, part), part)
+        wide[0, rows, :] = small[owner].astype(F32)[:part]
+
+    loop(small.shape[0], body)
+    weight[...] = wide[0].astype(BF16)
+
+
+def norm_places(norms, lane_rows):
     row = 0
-    for norm, rows in zip((tnorm, lnorm), lane_rows):
+    for norm, rows in zip(norms, lane_rows):
         for i in range(4):
             for j in range(rows):
                 lanes = min(128, norm.shape[1] - 128 * j)
-                norm[i : i + 1, 128 * j : 128 * j + lanes] = norm_sum[row : row + 1, :lanes]
+                yield row, lanes, norm, i, 128 * j
                 row += 1
 
 
-def pack_grads(small, planes, part, lane_rows, wide, gtnorm, glnorm, norm_sum):
+def unpack_second(small, part, lane_rows, weights, wide, norms, norm_sum):
     norm_sum[...] = jnp.zeros_like(norm_sum)
-    row = 0
-    for norm, rows in zip((gtnorm, glnorm), lane_rows):
-        for i in range(4):
-            for j in range(rows):
-                lanes = min(128, norm.shape[1] - 128 * j)
-                norm_sum[row : row + 1, :lanes] = norm[i : i + 1, 128 * j : 128 * j + lanes]
-                row += 1
-    tail = small.shape[-2] - 3 * part - norm_sum.shape[0]
-
+
+    def body(owner):
+        block = small[owner].astype(F32)
+        rows = pl.ds(pl.multiple_of(owner * part, part), part)
+        wide[1, rows, :] = block[:part]
+        wide[2, rows, :] = block[part : 2 * part]
+        norm_sum[...] += block[2 * part : 2 * part + norm_sum.shape[0]]
+
+    loop(small.shape[0], body)
+    for i, weight in enumerate(weights):
+        weight[...] = wide[1 + i].astype(BF16)
+    for row, lanes, norm, i, lane in norm_places(norms, lane_rows):
+        norm[i : i + 1, lane : lane + lanes] = norm_sum[row : row + 1, :lanes]
+
+
+def padded(pieces, rows):
+    tail = rows - sum(piece.shape[0] for piece in pieces)
+    if tail:
+        pieces = [*pieces, jnp.zeros((tail, pieces[0].shape[1]), F32)]
+    return jnp.concatenate(pieces, axis=0).astype(BF16)
+
+
+def pack_first(small, part, wide):
     def body(owner):
         rows = pl.ds(pl.multiple_of(owner * part, part), part)
-        pieces = [wide[i, rows, :] for i in range(3)] + [norm_sum[...]]
-        if tail:
-            pieces.append(jnp.zeros((tail, small.shape[-1]), F32))
-        block = jnp.concatenate(pieces, axis=0).astype(BF16)
-        small[owner // (2 * planes), lax.rem(owner // 2, planes), lax.rem(owner, 2)] = block
-
-    loop(4 * planes * 2, body)
-
-
-def spaced(tasks, first, last):
-    by_index = {}
-    for i, task in enumerate(tasks):
-        place = first + (last - first) * i // max(len(tasks) - 1, 1)
-        by_index.setdefault(place, []).append(task)
-    return by_index
-
-
-def heads_beside(body, by_index):
-    def step(head):
-        for place, tasks in sorted(by_index.items()):
-
-            def run(tasks=tasks):
-                for task in tasks:
-                    task()
-
-            pl.when(head == place)(run)
-        body(head)
-
-    loop(HEADS, step)
+        small[owner] = padded([wide[0, rows, :]], small.shape[1])
+
+    loop(small.shape[0], body)
+
+
+def pack_second(small, part, lane_rows, wide, norms, norm_sum):
+    norm_sum[...] = jnp.zeros_like(norm_sum)
+    for row, lanes, norm, i, lane in norm_places(norms, lane_rows):
+        norm_sum[row : row + 1, :lanes] = norm[i : i + 1, lane : lane + lanes]
+
+    def body(owner):
+        rows = pl.ds(pl.multiple_of(owner * part, part), part)
+        pieces = [wide[1, rows, :], wide[2, rows, :], norm_sum[...]]
+        small[owner] = padded(pieces, small.shape[1])
+
+    loop(small.shape[0], body)
+
+
+def due(plan, engine, slot):
+    return [
+        functools.partial(getattr(engine, step), *args) for at_slot, step, *args in plan if at_slot == slot
+    ]
+
+
+def move_on(plan, engine, slot):
+    for task in due(plan, engine, slot):
+        task()
+
+
+def move_on_at(plan, engine, first, count, index):
+    for i in range(count):
+        tasks = due(plan, engine, first + i)
+
+        def run(tasks=tasks):
+            for task in tasks:
+                task()
+
+        if tasks:
+            pl.when(index == i)(run)
 
 
 def whole_kernel(planes, dims, scales, chunks, part, lpart, *refs):
     (
-        lengths, x, y, gx, gy, own, own_small,
-        text_out, layout_out, dx, dy, gown_attn, gown_up, gown_down, gown_small,
-        attn, up, down, small, lattn, lup, ldown, wide, norm_sum,
+        lengths, x, yt, gx, gyt, own, own_first, own_second,
+        text_out, layout_out, dx, dyt, gown_attn, gown_up, gown_down, gown_first, gown_second,
+        y, gy, attn, up, down, small_first, small_second, lattn, lup, ldown, wide, norm_sum,
         tnorm, lnorm, gtnorm, glnorm,
         qkv_t, qkv_l, ctx_tt, ctx_tl, ctx_t, ctx_l, act_t, act_l, slope_t, slope_l,
         dhid_t, dhid_l, hat_t, hat_l, low_t, low_l, dlow_t, dlow_l, rate_t, rate_l, lse,
@@ -740,139 +964,183 @@
     length = lengths[0]
     half_rows = part // 2
 
-    def text_place(whole, half):
+    def owner_of(pair, plane, core):
+        return (pair * planes + plane) * 2 + core
+
+    def text_unit(whole, first, rows, order, z_apart):
         def place(pair, plane, core):
-            owner = (pair * planes + plane) * 2 + core
-            first = pl.multiple_of(owner * part + half * half_rows, half_rows)
-            return whole.at[pl.ds(first, half_rows), :]
-
-        return place
-
-    def small_place(whole):
-        return lambda pair, plane, core: whole.at[pair, plane, core]
+            row = owner_of(pair, plane, core) * part + first
+            return whole.at[pl.ds(pl.multiple_of(row, 16), rows), :]
+
+        return {
+            "place": place,
+            "sized": lambda count: whole.at[pl.ds(0, count * rows), :],
+            "order": order,
+            "z_last": z_apart,
+            "z_first": z_apart,
+        }
+
+    def small_unit(whole, order, z_apart):
+        return {
+            "place": lambda *block: whole.at[owner_of(*block)],
+            "sized": lambda count: whole.at[pl.ds(0, count)],
+            "order": order,
+            "z_last": z_apart,
+            "z_first": z_apart,
+        }
 
     gunits, sunits = [], []
-    for i, (whole, result) in enumerate(((attn, gown_attn), (up, gown_up), (down, gown_down))):
-        for half in (0, 1):
-            place = text_place(whole, half)
-            gunits.append({"own": own.at[i, half], "place": place, "order": half})
-            at_held = 4 * len(sunits)
-            sunits.append({"place": place, "order": half, "result": result.at[half]})
-            sunits[-1].update(zip(("core", "far", "near", "z"), held[at_held : at_held + 4]))
-    gunits.append({"own": own_small, "place": small_place(small), "order": 0})
-    sunits.append({"place": small_place(small), "order": 1, "result": gown_small})
-    sunits[-1].update(zip(("core", "far", "near", "z"), held[24:28]))
-    ATTN, UP, DOWN, SMALL = (0, 1), (2, 3), (4, 5), 6
+    texts = ((attn, gown_attn), (up, gown_up), (down, gown_down))
+    for which, first, rows, *way in text_cuts(part):
+        unit = text_unit(texts[which][0], first, rows, *way)
+        gunits.append({"own": own.at[which, pl.ds(first, rows), :], **unit})
+        sunits.append({"result": texts[which][1].at[pl.ds(first, rows), :], **unit})
+    for whole, source, result, way in (
+        (small_first, own_first, gown_first, (0, False)),
+        (small_second, own_second, gown_second, (1, SECOND_APART)),
+    ):
+        gunits.append({"own": source, **small_unit(whole, *way)})
+        sunits.append({"result": result, **small_unit(whole, *way)})
+    for i, unit in enumerate(sunits):
+        unit.update(zip(("core", "far", "near", "z"), held[4 * i : 4 * i + 4]))
+    for i, unit in enumerate(gunits):
+        unit["keep_sem"] = local_sem.at[i]
+    ATTN, UP, DOWN, FIRST, SECOND = (0, 1), (2, 3), (4, 5), (6,), (7,)
 
     entry_barrier(planes)
     gather = Gather(planes, gunits, gsend, grecv)
     scatter = Scatter(planes, sunits, ssend, srecv)
-    here = (gather.pair, gather.plane, gather.core)
-    keeps = [
-        pltpu.make_async_copy(unit["own"], unit["place"](*here), local_sem.at[i])
-        for i, unit in enumerate(gunits)
-    ]
-    for keep in keeps:
-        keep.start()
-
-    def task(step, *args):
-        return lambda: step(*args)
-
     def every(step, units, *args):
         for unit in units:
             step(unit, *args)
 
-    first = (*ATTN, SMALL)
-    every(gather.launch, first)
+    def forth(slot):
+        move_on(GATHER_PLAN, gather, slot)
+
+    def back(slot):
+        move_on(SCATTER_PLAN, scatter, slot)
+
+    start = (*ATTN, *FIRST)
+    every(gather.launch, start)
+    for unit in range(len(gunits)):
+        gather.keep(unit).start()
+    y[...] = yt[...].T
+    gy[...] = gyt[...].T
     for distance in range(1, planes):
-        every(gather.along, first, distance)
-    every(gather.launch, UP)
-    every(gather.from_near, first)
-    for distance in range(1, planes):
-        every(gather.along, UP, distance)
-    every(gather.from_far, first)
-    every(gather.from_core, first)
-    for unit in first:
-        keeps[unit].wait()
-
-    unpack_gathered(
-        small, planes, lpart, lane_rows, (lattn, lup, ldown), wide, tnorm, lnorm, norm_sum
-    )
+        every(gather.along, start, distance)
+    every(gather.from_near, start)
+    forth(0)
+    every(gather.from_far, start)
+    forth(1)
+    every(gather.from_core, start)
+    forth(2)
+    unpack_first(small_first, lpart, lattn, wide)
     project_heads(y, lattn, qkv_l, scales[1], chunks[1])
+    forth(3)
     project_heads(x, attn, qkv_t, scales[0], chunks[0])
-    early = [task(every, gather.launch, DOWN), *(task(gather.from_near, unit) for unit in UP)]
-    early += [task(every, gather.along, DOWN, distance) for distance in range(1, planes)]
-    late = spaced(early, 0, 5)
-    late[HEADS - 2] = [task(gather.from_far, UP[0])]
-    late[HEADS - 1] = [task(gather.from_far, UP[1])]
-    heads_beside(
-        lambda h: attend_head(h, length, qkv_t, qkv_l, ctx_tt, ctx_tl, lse, dims, widths), late
-    )
-    every(gather.from_near, DOWN)
+
+    def attend(head):
+        move_on_at(GATHER_PLAN, gather, 4, HEADS, head)
+        attend_head(head, length, qkv_t, qkv_l, ctx_tt, ctx_tl, lse, dims, widths)
+
+    loop(HEADS, attend)
+    forth(16)
+    every(gather.from_core, SECOND)
+    unpack_second(small_second, lpart, lane_rows, (lup, ldown), wide, (tnorm, lnorm), norm_sum)
     nothing = lambda i, block: None
+    stream_first(x, ctx_tt, ctx_t, attn, tnorm, dhid_t, hat_t, rate_t, low_t)
+    forth(17)
     stream_first(y, ctx_tl, ctx_l, lattn, lnorm, dhid_l, hat_l, rate_l, low_l)
+    forth(18)
     stream_up(low_l, lup, act_l, slope_l, chunks[1])
+    forth(19)
+    every(gather.from_core, UP)
+    stream_up(low_t, up, act_t, slope_t, chunks[0])
+    forth(20)
     stream_down(act_l, ldown, dhid_l, chunks[1])
-    stream_second(gy, lnorm, dhid_l, hat_l, layout_out, dhid_l, dlow_l, glnorm)
-    every(gather.from_far, DOWN)
-    stream_inner_back(
-        low_l, dlow_l, lup, ldown, act_l, slope_l, dhid_l, wide.at[1], wide.at[2], chunks[1], nothing
-    )
-    stream_first_back(
-        lnorm, hat_l, rate_l, dhid_l, dlow_l, ctx_l, lattn, ctx_tl, wide.at[0], glnorm
-    )
-    stream_first(x, ctx_tt, ctx_t, attn, tnorm, dhid_t, hat_t, rate_t, low_t)
-    every(gather.from_core, UP)
-    for unit in UP:
-        keeps[unit].wait()
-    stream_up(low_t, up, act_t, slope_t, chunks[0])
+    stream_second(gy, lnorm, dhid_l, hat_l, gy, dhid_l, dlow_l, glnorm)
+    layout_out[...] = gy[...].T
+    forth(21)
     every(gather.from_core, DOWN)
-    for unit in DOWN:
-        keeps[unit].wait()
     stream_down(act_t, down, dhid_t, chunks[0])
     stream_second(gx, tnorm, dhid_t, hat_t, text_out, dhid_t, dlow_t, gtnorm)
     every(gather.drain, range(len(gunits)))
 
     by_chunk = chunks[0] // (2 * part)
-
-    def ready(units):
-        return lambda i, block: every(scatter.launch, units, i * by_chunk, by_chunk)
+    by_pair = planes // by_chunk
+    pair_chunks = 4 * by_pair
+    inner_units = (*UP, *DOWN)
+
+    def chunk_of(i):
+        return scatter.turn(i // by_pair) * by_pair + lax.rem(i, by_pair)
+
+    def planes_of(i):
+        return [lax.rem(i, by_pair) * by_chunk + j for j in range(by_chunk)]
+
+    def inner_ready(i, block):
+        every(scatter.launch, inner_units, scatter.turn(i // by_pair), planes_of(i))
+        move_on_at(SCATTER_PLAN, scatter, 0, pair_chunks, i)
 
     stream_inner_back(
-        low_t, dlow_t, up, down, act_t, slope_t, dhid_t, up, down, chunks[0], ready((*UP, *DOWN))
-    )
+        low_t, dlow_t, up, down, act_t, slope_t, dhid_t, up, down, chunks[0], inner_ready, chunk_of
+    )
+    back(8)
+    stream_inner_back(
+        low_l, dlow_l, lup, ldown, act_l, slope_l, dhid_l, wide.at[1], wide.at[2], chunks[1], nothing
+    )
+    back(9)
+    stream_first_back(
+        lnorm, hat_l, rate_l, dhid_l, dlow_l, ctx_l, lattn, ctx_tl, wide.at[0], glnorm
+    )
+    back(10)
     stream_first_back(tnorm, hat_t, rate_t, dhid_t, dlow_t, ctx_t, attn, ctx_tt, attn, gtnorm)
-    every(scatter.launch, ATTN, 3 * planes, planes)
-    every(scatter.from_core, (*UP, *DOWN))
-    heads_beside(
-        lambda h: attend_head_back(
-            h, length, qkv_t, qkv_l, ctx_tt, ctx_tl, lse, qkv_t, qkv_l, dims, widths, scales
-        ),
-        {HEADS - 3: [task(scatter.from_far, UP[0])], HEADS - 2: [task(scatter.from_far, UP[1])]},
-    )
-    project_back(y, lattn, qkv_l, dhid_l, dy, wide.at[0], chunks[1], nothing)
-    pack_grads(small, planes, lpart, lane_rows, wide, gtnorm, glnorm, norm_sum)
-    scatter.launch(SMALL, 0, 4 * planes)
-    project_back(x, attn, qkv_t, dhid_t, dx, attn, chunks[0], ready(ATTN))
-    every(scatter.from_far, DOWN)
-    every(scatter.from_core, first)
-    every(scatter.from_near, UP)
-    every(scatter.from_near, DOWN)
-    every(scatter.from_z, UP)
-    every(scatter.from_z, DOWN)
-    every(scatter.finish, (*UP, *DOWN))
-    every(scatter.from_far, first)
-    every(scatter.from_near, first)
-    every(scatter.from_z, first)
-    every(scatter.finish, first)
+    every(scatter.launch, ATTN, 3)
+    pack_second(small_second, lpart, lane_rows, wide, (gtnorm, glnorm), norm_sum)
+    for pair in range(4):
+        every(scatter.launch, SECOND, pair)
+    back(11)
+
+    def attend_back(head):
+        move_on_at(SCATTER_PLAN, scatter, 12, HEADS, head)
+        attend_head_back(
+            head, length, qkv_t, qkv_l, ctx_tt, ctx_tl, lse, qkv_t, qkv_l, dims, widths, scales
+        )
+
+    loop(HEADS, attend_back)
+    back(24)
+    project_back(y, lattn, qkv_l, dhid_l, y, wide.at[0], chunks[1], nothing)
+    dyt[...] = y[...].T
+    pack_first(small_first, lpart, wide)
+    for pair in range(4):
+        every(scatter.launch, FIRST, pair)
+    back(25)
+
+    def attn_ready(i, block):
+        every(scatter.launch, ATTN, i // by_pair, planes_of(i))
+        move_on_at(SCATTER_PLAN, scatter, 26, 3 * by_pair, i)
+
+    project_back(x, attn, qkv_t, dhid_t, dx, attn, chunks[0], attn_ready)
+    back(32)
     every(scatter.drain, range(len(sunits)))
 
 
-def whole_layer(planes, x, y, lengths, gx, gy, own, own_small, lpart, linner):
+def text_cuts(part):
+    half = part // 2
+    return (
+        (0, 0, half, 0, False),
+        (0, half, half, 1, False),
+        (1, 0, half, 0, False),
+        (1, half, half, 1, False),
+        (2, 0, half, 0, False),
+        (2, half, half, 1, False),
+    )
+
+
+def whole_layer(planes, x, yt, lengths, gx, gyt, own, own_first, own_second, lpart, linner):
     rows, width = x.shape
-    lwidth = y.shape[1]
+    lwidth = yt.shape[0]
     owners = 4 * planes * 2
-    part = 2 * own.shape[2]
+    part = own.shape[1]
     inner = owners * part
     dims = (width // HEADS, lwidth // HEADS)
     scales = tuple(float(dim) ** -0.5 for dim in dims)
@@ -881,20 +1149,24 @@
     smem = pl.BlockSpec(memory_space=pltpu.SMEM)
     like = jax.ShapeDtypeStruct
     norm_count = 4 * sum(norm_rows((width, lwidth)))
-    small = (4, planes, 2, *own_small.shape)
 
     def both(shape_of, dtype):
         return [pltpu.VMEM(shape_of(width, inner), dtype), pltpu.VMEM(shape_of(lwidth, linner), dtype)]
 
     held = []
-    for _ in range(6):
-        held += Scatter.buffers(planes, own.shape[2:], BF16)
-    held += Scatter.buffers(planes, own_small.shape, BF16)
+    for _, _, cut, _, z_apart in text_cuts(part):
+        held += Scatter.buffers(planes, (cut, width), z_apart)
+    for own_small, z_apart in ((own_first, False), (own_second, SECOND_APART)):
+        held += Scatter.buffers(planes, own_small.shape, z_apart)
+    units = len(held) // 4
     scratch = [
+        pltpu.VMEM((rows, lwidth), BF16),
+        pltpu.VMEM((rows, lwidth), BF16),
         pltpu.VMEM((inner, width), BF16),
         pltpu.VMEM((inner, width), BF16),
         pltpu.VMEM((inner, width), BF16),
-        pltpu.VMEM(small, BF16),
+        pltpu.VMEM((owners, *own_first.shape), BF16),
+        pltpu.VMEM((owners, *own_second.shape), BF16),
         pltpu.VMEM((linner, lwidth), BF16),
         pltpu.VMEM((linner, lwidth), BF16),
         pltpu.VMEM((linner, lwidth), BF16),
@@ -914,30 +1186,62 @@
         *both(lambda w, f: (rows, 1), F32),
         pltpu.VMEM((HEADS, 1, rows), F32),
         *held,
-        pltpu.SemaphoreType.DMA((7,)),
-        pltpu.SemaphoreType.DMA((7, Gather.slots(planes))),
-        pltpu.SemaphoreType.DMA((7, owners)),
-        pltpu.SemaphoreType.DMA((7, Scatter.slots(planes))),
-        pltpu.SemaphoreType.DMA((7, Scatter.slots(planes))),
+        pltpu.SemaphoreType.DMA((units,)),
+        pltpu.SemaphoreType.DMA((units, Gather.send_slots(planes))),
+        pltpu.SemaphoreType.DMA((units, Gather.arrival_slots(planes))),
+        pltpu.SemaphoreType.DMA((units, Scatter.send_slots(planes))),
+        pltpu.SemaphoreType.DMA((units, Scatter.arrival_slots(planes))),
     ]
     return pl.pallas_call(
         functools.partial(whole_kernel, planes, dims, scales, (384, 192), part, lpart),
         out_shape=[
             like(x.shape, BF16),
-            like(y.shape, BF16),
+            like(yt.shape, BF16),
             like(x.shape, BF16),
-            like(y.shape, BF16),
+            like(yt.shape, BF16),
             *[like(own.shape[1:], F32)] * 3,
-            like(own_small.shape, F32),
+            like(own_first.shape, F32),
+            like(own_second.shape, F32),
         ],
-        in_specs=[smem] + [vmem] * 4 + [anywhere] * 2,
-        out_specs=[vmem] * 8,
+        in_specs=[smem] + [vmem] * 4 + [anywhere] * 3,
+        out_specs=[vmem] * 9,
         scratch_shapes=scratch,
         compiler_params=pltpu.CompilerParams(
             collective_id=0, has_side_effects=True, vmem_limit_bytes=67043328
         ),
         name="whole_layer",
-    )(lengths, x, y, gx, gy, own, own_small)
+    )(lengths, x, yt, gx, gyt, own, own_first, own_second)
+
+
+def results_kernel(cuts, *refs):
+    count = len(cuts)
+    sources, rest = refs[: -2 * count - 2], refs[-2 * count - 2 :]
+    targets, held, (in_sem, out_sem) = rest[:count], rest[count : 2 * count], rest[2 * count :]
+    takes, puts = [], []
+    for i, (which, rows, lanes) in enumerate(cuts):
+        source = sources[which].at[pl.ds(*rows), pl.ds(0, lanes)]
+        takes.append(pltpu.make_async_copy(source, held[i], in_sem.at[i]))
+        puts.append(pltpu.make_async_copy(held[i], targets[i], out_sem.at[i]))
+        takes[i].start()
+    for take, put in zip(takes, puts):
+        take.wait()
+        put.start()
+    for put in puts:
+        put.wait()
+
+
+def results(arrays, cuts):
+    shapes = [((rows[1], lanes), arrays[which].dtype) for which, rows, lanes in cuts]
+    anywhere = pl.BlockSpec(memory_space=pl.ANY)
+    return pl.pallas_call(
+        functools.partial(results_kernel, cuts),
+        out_shape=[jax.ShapeDtypeStruct(*shape) for shape in shapes],
+        in_specs=[anywhere] * len(arrays),
+        out_specs=[anywhere] * len(cuts),
+        scratch_shapes=[pltpu.VMEM(*shape) for shape in shapes]
+        + [pltpu.SemaphoreType.DMA((len(cuts),))] * 2,
+        name="results",
+    )(*arrays)
 
 
 def pack_small(pieces, norm_part, multiple):
@@ -978,23 +1282,30 @@
     owners = lax.axis_size(AXES)
     text_part, part = down_text.shape[0], down_layout.shape[0]
     count = norm_params.shape[0]
-    own = jnp.stack([attn_text.T, up_text.T, down_text]).reshape(3, 2, text_part // 2, width)
+    own = jnp.stack([attn_text.T, up_text.T, down_text])
     first = lax.axis_index(AXES) * count
     spread = jnp.pad(norm_params, ((owners - 1) * count, (owners - 1) * count))
     spread = lax.dynamic_slice(spread, ((owners - 1) * count - first,), (owners * count,))
     lanes = lanes_of(spread, (width, lwidth))
     lanes = jnp.pad(lanes, ((0, 0), (0, lwidth - 128)))
-    small = jnp.concatenate([attn_layout.T, up_layout.T, down_layout, lanes], axis=0)
-    small = jnp.pad(small, ((0, -small.shape[0] % 16), (0, 0)))
-    text_out, layout_out, dx, dy, gattn, gup, gdown, gsmall = whole_layer(
-        planes, text_in, layout_in, lengths, grad_text, grad_layout, own, small,
+    own_first, own_second = (
+        jnp.pad(block, ((0, -block.shape[0] % 16), (0, 0)))
+        for block in (attn_layout.T, jnp.concatenate([up_layout.T, down_layout, lanes], axis=0))
+    )
+    arrays = whole_layer(
+        planes, text_in, layout_in.T, lengths, grad_text, grad_layout.T, own, own_first, own_second,
         part, owners * part,
     )
-    gattn, gup, gdown = (grad.reshape(text_part, width) for grad in (gattn, gup, gdown))
-    glattn, glup, gldown = (gsmall[i * part : (i + 1) * part] for i in range(3))
-    gnorm = gsmall[3 * part : 3 * part + lanes.shape[0], :128]
+    cuts = [(i, (0, array.shape[0]), array.shape[1]) for i, array in enumerate(arrays[:7])]
+    cuts += [(7, (0, part), lwidth), (8, (0, part), lwidth), (8, (part, part), lwidth)]
+    cuts += [(8, (2 * part, lanes.shape[0]), 128)]
+    text_out, layout_out, dx, dy, gattn, gup, gdown, glattn, glup, gldown, gnorm = results(
+        arrays, cuts
+    )
     gnorm = lax.dynamic_slice(flat_of(gnorm, (width, lwidth)), (first,), (count,))
-    return text_out, layout_out, dx, dy, gattn.T, gup.T, gdown, glattn.T, glup.T, gldown, gnorm
+    return (
+        text_out, layout_out.T, dx, dy.T, gattn.T, gup.T, gdown, glattn.T, glup.T, gldown, gnorm,
+    )
 
 
 def by_collectives(
@@ -1043,7 +1354,7 @@
 def solution(mesh):
     pairs, columns_on_axis = mesh.shape["dp"], mesh.shape["fsdp"]
     body = by_collectives
-    if pairs == 4 and columns_on_axis % 2 == 0 and columns_on_axis <= 8:
+    if pairs == 4 and columns_on_axis == 8:
         body = functools.partial(by_kernel, columns_on_axis // 2)
     rows, columns = P(AXES, None), P(None, AXES)
     split = P(AXES)

time: 230 us -> 196 us (0.85)
  Pallas kernels: 210 us -> 187 us
  local copies, waits for them, and re-layouts: 15.5 us -> 3.72 us
    pallas_call x1, Pallas kernels: 210 us -> 184 us  [whole_layer(): pl.pallas_call(functools.partial(whole_kernel, planes, dims, scales, (384...]
    unnamed x29 -> x4, local copies, waits for them, and re-layouts: 11 us -> 0.71 us
    pallas_call x0 -> x1, Pallas kernels: none -> 2.9 us  [results(): pl.pallas_call(functools.partial(results_kernel, cuts), out_shape=[jax.Sh...]
where the time goes in v4:
time: 196 us
  Pallas kernels  187 us (95%)
  other arithmetic  3.74 us (2%)
  local copies, waits for them, and re-layouts  3.72 us (2%)
    pallas_call x1, Pallas kernels, whole_layer(): pl.pallas_call(functools.partial(whole_kernel, planes, dims, scales, (384...  184 us

profile of v4, /device:TPU:0, one launch (start us, length us, event | category | flops | bytes accessed | tf_op | source)
XLA Modules:
  0.0 195.6 jit_solution(14324583383591530614)
XLA Ops:
  0.6 0.0 copy-start
  1.3 0.7 pad_dynamic-slice_fusion.1
  2.1 0.1 reshape.53
  2.2 0.7 fusion.3
  2.9 1.3 pad.16.refs_6_
  4.3 1.3 pad_maximum_fusion.1.refs_7_
  5.6 0.0 copy-done
  5.6 1.8 pad_maximum_fusion.refs_5_
  7.4 183.9 %whole_layer.1 = (bf16[512,768]{1,0:T(8,128)(2,1)}, bf16[192,512]{1,0:T(8,128)(2,1)}, bf16[512,768]{1,0:T(8,128)(2,1)}, bf16[192,512]{1,0:T(8,128)(2,1)}, f32[96...) custom-call(s32[1]{0:T(128)S(6)} %copy.23.refs_0_, ...), custom_call_target="tpu_custom_call" | custom-call | tf_op jit(solution)/shard_map/whole_layer/pallas_call | solution.py:1195
  191.3 2.9 %results.1 = (bf16[512,768]{1,0:T(8,128)(2,1)}, bf16[192,512]{1,0:T(8,128)(2,1)}, bf16[512,768]{1,0:T(8,128)(2,1)}, bf16[192,512]{1,0:T(8,128)(2,1)}, f32[96,768...) custom-call(bf16[512,768]{1,0:T(8,128)(2,1)} %get-tuple-element.31.r, ...), custom_call_target="tpu_custom_call" | custom-call | tf_op jit(solution)/shard_map/results/pallas_call | solution.py:1236
  194.2 0.0 copy-start.1
  194.2 0.7 copy-done.1
  195.0 0.1 reshape.56
  195.0 0.6 fusion.4
  (6 shorter events, 0.0 us)
Async XLA Ops:
  0.6 5.0 %copy-start = (bf16[96,768]{1,0:T(8,128)(2,1)S(1)}, bf16[96,768]{1,0:T(8,128)(2,1)}, u32[]{:S(2)}) copy-start(bf16[96,768]{1,0:T(8,128)(2,1)} %param.17) | copy-start | bytes 442372
  194.2 0.7 copy-start.1
